TPU v7x, 32 devices: a 4x4x1 block of a 4x4x8 slice. The times are simulated.
32 devices in a mesh: batch: 1 (over z), w: 4 (over y), h: 8 (over x, core).
Axes of the slice: x: 4, y: 4, z: 1, core: 2. Of those that a mesh axis runs over, the one named last changes fastest.
The devices are a block of a 4x4x8 slice.
Arguments:
- image: bfloat16 [256, 2048, 32, 1], P('batch', 'h', 'w')
- down_w1: bfloat16 [3, 3, 1, 64], replicated
- down_v1: float32 [3, 64], replicated
- refine_w1: bfloat16 [3, 3, 64, 64], replicated
- refine_v1: float32 [3, 64], replicated
- down_w2: bfloat16 [3, 3, 64, 128], replicated
- down_v2: float32 [3, 128], replicated
- refine_w2: bfloat16 [3, 3, 128, 128], replicated
- refine_v2: float32 [3, 128], replicated
- down_w3: bfloat16 [3, 3, 128, 256], replicated
- down_v3: float32 [3, 256], replicated
- refine_w3: bfloat16 [3, 3, 256, 256], replicated
- refine_v3: float32 [3, 256], replicated
Outputs:
- output: bfloat16 [256, 256, 4, 256], P('batch', 'h', 'w')
All inputs are finite; a program needn't handle non-finite values.
Results may differ from a plain program's by a relative error of at most 0.00374919.
Values are sent between devices in bfloat16 or wider.
A program may use at most 768 MiB of HBM per device.

v0:
```python
import jax
import jax.numpy as jnp
from jax import lax
from jax.sharding import PartitionSpec as P

NORM_GROUPS = 8
NORM_EPS = 1e-5


def shift_in(piece, axis_name, axis_size, from_lower):
    if axis_size == 1:
        return jnp.zeros_like(piece)
    if from_lower:
        send_pairs = [(source, source + 1) for source in range(axis_size - 1)]
    else:
        send_pairs = [(source + 1, source) for source in range(axis_size - 1)]
    return lax.ppermute(piece, axis_name, send_pairs)


def lower_halo(tile, row_count, col_count):
    above = shift_in(tile[:, -1:], "h", row_count, True)
    tall = jnp.concatenate([above, tile], axis=1)
    left = shift_in(tall[:, :, -1:], "w", col_count, True)
    return jnp.concatenate([left, tall], axis=2)


def both_halo(tile, row_count, col_count):
    above = shift_in(tile[:, -1:], "h", row_count, True)
    below = shift_in(tile[:, :1], "h", row_count, False)
    tall = jnp.concatenate([above, tile, below], axis=1)
    left = shift_in(tall[:, :, -1:], "w", col_count, True)
    right = shift_in(tall[:, :, :1], "w", col_count, False)
    return jnp.concatenate([left, tall, right], axis=2)


def norm_apply(summed, affine, totals, pixel_count, per_group):
    grp_mean = totals[0] / pixel_count
    grp_var = jnp.maximum(totals[1] / pixel_count - jnp.square(grp_mean), 0.0)
    inv_std = lax.rsqrt(grp_var + NORM_EPS)
    chan_scale = jnp.repeat(inv_std, per_group, axis=1) * affine[1]
    chan_shift = affine[2] - jnp.repeat(grp_mean * inv_std, per_group, axis=1) * affine[1]
    return jax.nn.relu(summed * chan_scale[:, None, None, :] + chan_shift[:, None, None, :]).astype(jnp.bfloat16)


def conv_norm(padded, kernel, affine, stride, spatial_devices):
    summed = lax.conv_general_dilated(padded, kernel, (stride, stride), "VALID", dimension_numbers=("NHWC", "HWIO", "NHWC"), preferred_element_type=jnp.float32) + affine[0]
    out_shape = summed.shape
    per_group = out_shape[3] // NORM_GROUPS
    pixel_count = out_shape[1] * out_shape[2] * spatial_devices * per_group
    part_sums = jnp.stack([jnp.sum(summed, axis=(1, 2)), jnp.sum(jnp.square(summed), axis=(1, 2))])
    part_sums = jnp.sum(part_sums.reshape(2, out_shape[0], NORM_GROUPS, per_group), axis=3)
    totals = lax.psum(part_sums, ("h", "w"))
    return norm_apply(summed, affine, totals, pixel_count, per_group)


def solution(mesh):
    row_count = mesh.shape["h"]
    col_count = mesh.shape["w"]
    spatial_devices = row_count * col_count
    act_spec = P("batch", "h", "w")

    def local_forward(tile, *params):
        current = tile
        for stage in range(3):
            down_w, down_v, refine_w, refine_v = params[4 * stage:4 * stage + 4]
            current = conv_norm(lower_halo(current, row_count, col_count), down_w, down_v, 2, spatial_devices)
            current = conv_norm(both_halo(current, row_count, col_count), refine_w, refine_v, 1, spatial_devices)
        return current

    return jax.shard_map(local_forward, mesh=mesh, in_specs=(act_spec,) + (P(),) * 12, out_specs=act_spec, check_vma=False)
```

profile of v0, /device:TPU:97, one launch (start us, length us, event | category | flops | bytes accessed | tf_op | source)
XLA Modules:
  0.0 991.4 jit_solution(18395903309117408478)
XLA Ops:
  0.0 4.6 copy.38
  4.6 4.6 collective-permute-start
  10.4 3.8 collective-permute-start.1
  15.0 4.5 collective-permute-done.1
  19.4 15.2 %add_reduce_fusion.1 = (f32[256,64]{0,1:T(8,128)S(1)}, f32[256,64]{0,1:T(8,128)S(1)}, f32[256,128,4,64]{0,3,2,1:T(8,128)}) fusion(f32[64]{0:T(128)S(1)} %get-tuple-element.55, bf16[3,3,1,64]{3,1,2,0:T(4,128)(2,1)} %param.14, bf16[256,256,8,1]{0,3,2,1:T(2,128)(2,1)S(1)} %copy.38, bf16[256,1,8,1]{0,3,2,1:T(2,128)(2,1)S(1)} %collective-permute-done, ...), kind=kOutput, calls=%fused_computation.5 | convolution fusion | flops 188069376 | bytes 34871168 | tf_op jit(solution)/shard_map/conv_general_dilated | solution.py:46
  34.7 47.8 %psum.42 = f32[2,256,8]{1,2,0:T(8,128)S(1)} all-reduce(f32[2,256,8]{1,2,0:T(8,128)S(1)} %maximum_reduce_fusion.4), channel_id=1, replica_groups=mesh['batch'=1,'w'=4,'h'=8] {'h','w'}, use_global_device_ids=true, to_apply=%region_3.0 | all-reduce | flops 4096 | bytes 32768 | tf_op jit(solution)/shard_map/psum | solution.py:52
  82.6 13.8 %maximum_convert_fusion.1 = bf16[256,128,4,64]{0,3,2,1:T(8,128)(2,1)S(1)} fusion(f32[256,128,4,64]{0,3,2,1:T(8,128)} %get-tuple-element.69, f32[256,64]{0,1:T(8,128)S(1)} %get-tuple-element.68, f32[256,64]{0,1:T(8,128)S(1)} %get-tuple-element.67, f32[64]{0:T(128)S(1)} %get-tuple-element.55), kind=kLoop, calls=%fused_computation.2 | loop fusion | flops 41943040 | bytes 50462976 | tf_op jit(solution)/shard_map/convert_element_type | solution.py:42
  96.5 2.5 collective-permute-start.2
  99.1 2.1 collective-permute-start.3
  101.2 4.3 collective-permute-done.3
  107.2 2.1 collective-permute-start.4
  110.7 87.6 %collective-permute-done.4 = bf16[256,130,1,64]{0,3,2,1:T(8,128)(2,1)S(1)} collective-permute-done((bf16[256,130,1,64]{0,3,2,1:T(8,128)(2,1)S(1)}, bf16[256,130,1,64]{0,3,2,1:T(8,128)(2,1)S(1)}, u32[]{:S(2)}, u32[]{:S(2)}) %collective-permute-start.4) | collective-permute-done | bytes 4259872 | tf_op jit(solution)/shard_map/ppermute | solution.py:17
  198.2 4.4 collective-permute-done.5
  202.7 2.1 copy-done.6
  204.7 34.3 %add_reduce_fusion = (f32[256,64]{0,1:T(8,128)S(1)}, f32[256,64]{0,1:T(8,128)S(1)}, f32[256,128,4,64]{0,3,2,1:T(8,128)}) fusion(f32[64]{0:T(128)S(1)} %get-tuple-element.52, bf16[3,3,64,64]{3,2,1,0:T(8,128)(2,1)S(1)} %copy-done.10, bf16[256,130,1,64]{0,3,2,1:T(8,128)(2,1)} %copy-done.6, bf16[256,1,4,64]{0,3,2,1:T(8,128)(2,1)S(1)} %collective-permute-done.3, ...), kind=kOutput, calls=%fused_computation.4 | convolution fusion | flops 9748316160 | bytes 59318528 | tf_op jit(solution)/shard_map/conv_general_dilated | solution.py:46
  239.0 47.0 %psum.43 = f32[2,256,8]{1,2,0:T(8,128)S(1)} all-reduce(f32[2,256,8]{1,2,0:T(8,128)S(1)} %maximum_reduce_fusion.5), channel_id=1, replica_groups=mesh['batch'=1,'w'=4,'h'=8] {'h','w'}, use_global_device_ids=true, to_apply=%region_7.8 | all-reduce | flops 4096 | bytes 32768 | tf_op jit(solution)/shard_map/psum | solution.py:52
  286.1 13.9 %maximum_convert_fusion = bf16[256,128,4,64]{0,3,2,1:T(8,128)(2,1)S(1)} fusion(f32[256,128,4,64]{0,3,2,1:T(8,128)} %get-tuple-element.70, f32[256,64]{0,1:T(8,128)S(1)} %get-tuple-element.66, f32[256,64]{0,1:T(8,128)S(1)} %get-tuple-element.65, f32[64]{0:T(128)S(1)} %get-tuple-element.52), kind=kLoop, calls=%fused_computation | loop fusion | flops 41943040 | bytes 50462976 | tf_op jit(solution)/shard_map/convert_element_type | solution.py:42
  300.1 2.1 collective-permute-start.6
  304.5 2.7 collective-permute-start.7
  307.2 89.4 %collective-permute-done.7 = bf16[256,129,1,64]{0,3,2,1:T(8,128)(2,1)S(1)} collective-permute-done((bf16[256,129,1,64]{0,3,2,1:T(8,128)(2,1)S(1)}, bf16[256,129,1,64]{0,3,2,1:T(8,128)(2,1)S(1)}, u32[]{:S(2)}, u32[]{:S(2)}) %collective-permute-start.7) | collective-permute-done | bytes 4227104 | tf_op jit(solution)/shard_map/ppermute | solution.py:17
  396.6 1.9 copy-done.7
  398.5 15.4 %add_reduce_fusion.3 = (f32[256,128]{1,0:T(8,128)S(1)}, f32[256,128]{1,0:T(8,128)S(1)}, f32[256,64,2,128]{3,0,2,1:T(8,128)}) fusion(f32[128]{0:T(128)S(1)} %get-tuple-element.49, bf16[3,3,64,128]{3,2,1,0:T(8,128)(2,1)S(1)} %copy-done.11, bf16[256,128,4,64]{0,3,2,1:T(8,128)(2,1)S(1)} %maximum_convert_fusion, ...), kind=kOutput, calls=%fused_computation.37 | convolution fusion | flops 4869685248 | bytes 38322688 | tf_op jit(solution)/shard_map/conv_general_dilated | solution.py:46
  414.2 46.5 %psum.44 = f32[2,256,8]{1,2,0:T(8,128)S(1)} all-reduce(f32[2,256,8]{1,2,0:T(8,128)S(1)} %maximum_reduce_fusion.2), channel_id=1, replica_groups=mesh['batch'=1,'w'=4,'h'=8] {'h','w'}, use_global_device_ids=true, to_apply=%region_11.12 | all-reduce | flops 4096 | bytes 32768 | tf_op jit(solution)/shard_map/psum | solution.py:52
  461.0 7.7 maximum_convert_fusion.3
  468.8 3.0 collective-permute-start.8
  471.7 2.0 collective-permute-start.9
  473.7 4.3 collective-permute-done.9
  483.5 89.3 %collective-permute-done.10 = bf16[256,66,1,128]{3,0,2,1:T(8,128)(2,1)S(1)} collective-permute-done((bf16[256,66,1,128]{3,0,2,1:T(8,128)(2,1)S(1)}, bf16[256,66,1,128]{3,0,2,1:T(8,128)(2,1)S(1)}, u32[]{:S(2)}, u32[]{:S(2)}) %collective-permute-start.10) | collective-permute-done | bytes 4325408 | tf_op jit(solution)/shard_map/ppermute | solution.py:17
  572.7 4.4 collective-permute-done.11
  577.1 22.4 %add_reduce_fusion.2 = (f32[256,128]{1,0:T(8,128)S(1)}, f32[256,128]{1,0:T(8,128)S(1)}, f32[256,64,2,128]{3,0,2,1:T(8,128)}) fusion(f32[128]{0:T(128)S(1)} %get-tuple-element.46, bf16[3,3,128,128]{3,2,1,0:T(8,128)(2,1)S(1)} %copy-done.9, bf16[256,66,1,128]{3,0,2,1:T(8,128)(2,1)S(1)} %collective-permute-done.11, ...), kind=kOutput, calls=%fused_computation.36 | convolution fusion | flops 9714991104 | bytes 34636288 | tf_op jit(solution)/shard_map/conv_general_dilated | solution.py:46
  599.8 47.1 %psum.45 = f32[2,256,8]{1,2,0:T(8,128)S(1)} all-reduce(f32[2,256,8]{1,2,0:T(8,128)S(1)} %maximum_reduce_fusion.3), channel_id=1, replica_groups=mesh['batch'=1,'w'=4,'h'=8] {'h','w'}, use_global_device_ids=true, to_apply=%region_15.16 | all-reduce | flops 4096 | bytes 32768 | tf_op jit(solution)/shard_map/psum | solution.py:52
  647.2 7.6 maximum_convert_fusion.2
  654.8 2.1 collective-permute-start.12
  659.2 2.7 collective-permute-start.13
  661.9 90.1 %collective-permute-done.13 = bf16[256,65,1,128]{3,0,2,1:T(8,128)(2,1)S(1)} collective-permute-done((bf16[256,65,1,128]{3,0,2,1:T(8,128)(2,1)S(1)}, bf16[256,65,1,128]{3,0,2,1:T(8,128)(2,1)S(1)}, u32[]{:S(2)}, u32[]{:S(2)}) %collective-permute-start.13) | collective-permute-done | bytes 4259872 | tf_op jit(solution)/shard_map/ppermute | solution.py:17
  752.0 8.2 add_reduce_fusion.5
  760.5 46.8 %psum.46 = f32[2,256,8]{1,2,0:T(8,128)S(1)} all-reduce(f32[2,256,8]{1,2,0:T(8,128)S(1)} %maximum_reduce_fusion), channel_id=1, replica_groups=mesh['batch'=1,'w'=4,'h'=8] {'h','w'}, use_global_device_ids=true, to_apply=%region_19.20 | all-reduce | flops 4096 | bytes 32768 | tf_op jit(solution)/shard_map/psum | solution.py:52
  807.7 4.8 maximum_convert_fusion.5
  812.6 2.7 collective-permute-start.14
  815.2 2.0 collective-permute-start.15
  817.2 4.3 collective-permute-done.15
  822.2 2.0 collective-permute-start.16
  825.5 91.9 %collective-permute-done.16 = bf16[256,34,1,256]{3,0,2,1:T(8,128)(2,1)S(1)} collective-permute-done((bf16[256,34,1,256]{3,0,2,1:T(8,128)(2,1)S(1)}, bf16[256,34,1,256]{3,0,2,1:T(8,128)(2,1)S(1)}, u32[]{:S(2)}, u32[]{:S(2)}) %collective-permute-start.16) | collective-permute-done | bytes 4456480 | tf_op jit(solution)/shard_map/ppermute | solution.py:17
  917.4 4.4 collective-permute-done.17
  921.8 12.3 %add_reduce_fusion.4 = (f32[256,256]{1,0:T(8,128)S(1)}, f32[256,256]{1,0:T(8,128)S(1)}, f32[256,32,1,256]{3,0,2,1:T(8,128)}) fusion(f32[256]{0:T(256)S(1)} %bitcast.207, bf16[3,3,256,256]{3,2,1,0:T(8,128)(2,1)S(1)} %copy-done, bf16[256,34,1,256]{3,0,2,1:T(8,128)(2,1)S(1)} %collective-permute-done.17, ...), kind=kOutput, calls=%fused_computation.59 | convolution fusion | flops 9698672640 | bytes 23462912 | tf_op jit(solution)/shard_map/conv_general_dilated | solution.py:46
  934.4 46.9 %psum.47 = f32[2,256,8]{1,2,0:T(8,128)S(1)} all-reduce(f32[2,256,8]{1,2,0:T(8,128)S(1)} %maximum_reduce_fusion.1), channel_id=1, replica_groups=mesh['batch'=1,'w'=4,'h'=8] {'h','w'}, use_global_device_ids=true, to_apply=%region_23.24 | all-reduce | flops 4096 | bytes 32768 | tf_op jit(solution)/shard_map/psum | solution.py:52
  981.8 4.8 maximum_convert_fusion.4
  986.6 4.4 copy.57
  (85 shorter events, 19.7 us)
Async XLA Ops:
  0.0 921.8 %copy-start = (bf16[3,3,256,256]{3,2,1,0:T(8,128)(2,1)S(1)}, bf16[3,3,256,256]{3,2,1,0:T(8,128)(2,1)}, u32[]{:S(2)}) copy-start(bf16[3,3,256,256]{3,2,1,0:T(8,128)(2,1)} %param.24) | copy-start | bytes 3538948
  4.6 5.4 collective-permute-start
  10.4 9.1 collective-permute-start.1
  96.5 4.7 collective-permute-start.2
  99.1 11.6 %copy-start.3 = (f32[3,64]{1,0:T(4,128)S(1)}, f32[3,64]{1,0:T(4,128)}, u32[]{:S(2)}) copy-start(f32[3,64]{1,0:T(4,128)} %param.17) | copy-start | bytes 2308
  99.1 105.7 %copy-start.10 = (bf16[3,3,64,64]{3,2,1,0:T(8,128)(2,1)S(1)}, bf16[3,3,64,64]{3,2,1,0:T(8,128)(2,1)}, u32[]{:S(2)}) copy-start(bf16[3,3,64,64]{3,2,1,0:T(8,128)(2,1)} %param.16) | copy-start | bytes 221188
  99.1 6.4 collective-permute-start.3
  107.2 91.0 %collective-permute-start.4 = (bf16[256,130,1,64]{0,3,2,1:T(8,128)(2,1)S(1)}, bf16[256,130,1,64]{0,3,2,1:T(8,128)(2,1)S(1)}, u32[]{:S(2)}, u32[]{:S(2)}) collective-permute-start(bf16[256,130,1,64]{0,3,2,1:T(8,128)(2,1)S(1)} %get-tuple-element.29), channel_id=1, source_target_pairs={{0,8},{8,16},{16,24},{1,9},{9,17},{17,25},{2,10},{10,18},{18,26},{... | collective-permute-start | bytes 12779528 | tf_op jit(solution)/shard_map/ppermute | solution.py:17
  109.3 93.3 %collective-permute-start.5 = (bf16[256,130,1,64]{0,3,2,1:T(8,128)(2,1)S(1)}, bf16[256,130,1,64]{0,3,2,1:T(8,128)(2,1)S(1)}, u32[]{:S(2)}, u32[]{:S(2)}) collective-permute-start(bf16[256,130,1,64]{0,3,2,1:T(8,128)(2,1)S(1)} %get-tuple-element.30), channel_id=1, source_target_pairs={{8,0},{16,8},{24,16},{9,1},{17,9},{25,17},{10,2},{18,10},{26,18},{... | collective-permute-start | bytes 12779528 | tf_op jit(solution)/shard_map/ppermute | solution.py:17
  202.7 2.1 copy-start.6
  300.1 7.1 copy-start.4
  300.1 98.4 %copy-start.11 = (bf16[3,3,64,128]{3,2,1,0:T(8,128)(2,1)S(1)}, bf16[3,3,64,128]{3,2,1,0:T(8,128)(2,1)}, u32[]{:S(2)}) copy-start(bf16[3,3,64,128]{3,2,1,0:T(8,128)(2,1)} %param.18) | copy-start | bytes 442372
  300.1 4.0 collective-permute-start.6
  304.5 92.1 %collective-permute-start.7 = (bf16[256,129,1,64]{0,3,2,1:T(8,128)(2,1)S(1)}, bf16[256,129,1,64]{0,3,2,1:T(8,128)(2,1)S(1)}, u32[]{:S(2)}, u32[]{:S(2)}) collective-permute-start(bf16[256,129,1,64]{0,3,2,1:T(8,128)(2,1)S(1)} %pad_maximum_fusion.6), channel_id=1, source_target_pairs={{0,8},{8,16},{16,24},{1,9},{9,17},{17,25},{2,10},{10,18},{18,26},{... | collective-permute-start | bytes 12681224 | tf_op jit(solution)/shard_map/ppermute | solution.py:17
  396.6 1.9 copy-start.7
  468.8 4.9 collective-permute-start.8
  471.7 6.3 collective-permute-start.9
  479.2 4.2 copy-start.5
  479.2 97.9 %copy-start.9 = (bf16[3,3,128,128]{3,2,1,0:T(8,128)(2,1)S(1)}, bf16[3,3,128,128]{3,2,1,0:T(8,128)(2,1)}, u32[]{:S(2)}) copy-start(bf16[3,3,128,128]{3,2,1,0:T(8,128)(2,1)} %param.20) | copy-start | bytes 884740
  480.3 92.4 %collective-permute-start.10 = (bf16[256,66,1,128]{3,0,2,1:T(8,128)(2,1)S(1)}, bf16[256,66,1,128]{3,0,2,1:T(8,128)(2,1)S(1)}, u32[]{:S(2)}, u32[]{:S(2)}) collective-permute-start(bf16[256,66,1,128]{3,0,2,1:T(8,128)(2,1)S(1)} %get-tuple-element.33), channel_id=1, source_target_pairs={{0,8},{8,16},{16,24},{1,9},{9,17},{17,25},{2,10},{10,18},{18,26},{... | collective-permute-start | bytes 12976136 | tf_op jit(solution)/shard_map/ppermute | solution.py:17
  481.9 95.2 %collective-permute-start.11 = (bf16[256,66,1,128]{3,0,2,1:T(8,128)(2,1)S(1)}, bf16[256,66,1,128]{3,0,2,1:T(8,128)(2,1)S(1)}, u32[]{:S(2)}, u32[]{:S(2)}) collective-permute-start(bf16[256,66,1,128]{3,0,2,1:T(8,128)(2,1)S(1)} %get-tuple-element.34), channel_id=1, source_target_pairs={{8,0},{16,8},{24,16},{9,1},{17,9},{25,17},{10,2},{18,10},{26,18},{... | collective-permute-start | bytes 12976136 | tf_op jit(solution)/shard_map/ppermute | solution.py:17
  654.8 7.1 copy-start.1
  654.8 97.2 %copy-start.8 = (bf16[3,3,128,256]{3,2,1,0:T(8,128)(2,1)S(1)}, bf16[3,3,128,256]{3,2,1,0:T(8,128)(2,1)}, u32[]{:S(2)}) copy-start(bf16[3,3,128,256]{3,2,1,0:T(8,128)(2,1)} %param.22) | copy-start | bytes 1769476
  654.8 4.0 collective-permute-start.12
  659.2 92.8 %collective-permute-start.13 = (bf16[256,65,1,128]{3,0,2,1:T(8,128)(2,1)S(1)}, bf16[256,65,1,128]{3,0,2,1:T(8,128)(2,1)S(1)}, u32[]{:S(2)}, u32[]{:S(2)}) collective-permute-start(bf16[256,65,1,128]{3,0,2,1:T(8,128)(2,1)S(1)} %pad_maximum_fusion.2), channel_id=1, source_target_pairs={{0,8},{8,16},{16,24},{1,9},{9,17},{17,25},{2,10},{10,18},{18,26},{... | collective-permute-start | bytes 12779528 | tf_op jit(solution)/shard_map/ppermute | solution.py:17
  807.7 17.7 %copy-start.2 = (f32[3,256]{1,0:T(4,128)S(1)}, f32[3,256]{1,0:T(4,128)}, u32[]{:S(2)}) copy-start(f32[3,256]{1,0:T(4,128)} %param.25) | copy-start | bytes 9220
  812.6 4.6 collective-permute-start.14
  815.2 6.3 collective-permute-start.15
  822.2 95.2 %collective-permute-start.16 = (bf16[256,34,1,256]{3,0,2,1:T(8,128)(2,1)S(1)}, bf16[256,34,1,256]{3,0,2,1:T(8,128)(2,1)S(1)}, u32[]{:S(2)}, u32[]{:S(2)}) collective-permute-start(bf16[256,34,1,256]{3,0,2,1:T(8,128)(2,1)S(1)} %pad_maximum_fusion.1), channel_id=1, source_target_pairs={{0,8},{8,16},{16,24},{1,9},{9,17},{17,25},{2,10},{10,18},{18,26},{... | collective-permute-start | bytes 13369352 | tf_op jit(solution)/shard_map/ppermute | solution.py:17
  824.1 97.7 %collective-permute-start.17 = (bf16[256,34,1,256]{3,0,2,1:T(8,128)(2,1)S(1)}, bf16[256,34,1,256]{3,0,2,1:T(8,128)(2,1)S(1)}, u32[]{:S(2)}, u32[]{:S(2)}) collective-permute-start(bf16[256,34,1,256]{3,0,2,1:T(8,128)(2,1)S(1)} %pad_maximum_fusion.1), channel_id=1, source_target_pairs={{8,0},{16,8},{24,16},{9,1},{17,9},{25,17},{10,2},{18,10},{26,18},{... | collective-permute-start | bytes 13369352 | tf_op jit(solution)/shard_map/ppermute | solution.py:17
where the time goes:
time: 1000 us; the launch traced here: 991 us
  waiting for transfers between devices  484 us (48%)
  blocking collectives  282 us (28%)
  matrix products  108 us (11%)
  other arithmetic  58.2 us (6%)
  starting transfers between devices  41.9 us (4%)
  local copies, waits for them, and re-layouts  16.8 us (2%)
    ppermute x18, waiting for transfers between devices, shift_in(): return lax.ppermute(piece, axis_name, send_pairs)  484 us
    psum x6, blocking collectives, conv_norm(): totals = lax.psum(part_sums, ('h', 'w'))  282 us
    conv_general_dilated x6, matrix products, conv_norm(): lax.conv_general_dilated(padded, kernel, (stride, stride), 'VALID', dimen...  108 us
    convert_element_type x6, other arithmetic, norm_apply(): jax.nn.relu(summed * chan_scale[:, None, None, :] + chan_shift[:, None, N...  52.6 us
    ppermute x18, starting transfers between devices, shift_in(): return lax.ppermute(piece, axis_name, send_pairs)  41.9 us
  transfers between devices with their start and end apart: 18, of which 15 were waited for; matrix products, arithmetic and copies ran while one was open for 0% of the time, Pallas kernels for 0%

commit v1 on v0

v1 whole, which is shorter than its diff:
```python
import jax
import jax.numpy as jnp
from jax import lax
from jax.sharding import PartitionSpec as P

NORM_GROUPS = 8
NORM_EPS = 1e-5


def conv_norm(inputs, kernel, affine, stride):
    pads = ((1, 0), (1, 0)) if stride == 2 else ((1, 1), (1, 1))
    summed = lax.conv_general_dilated(inputs, kernel, (stride, stride), pads, dimension_numbers=("NHWC", "HWIO", "NHWC"), preferred_element_type=jnp.float32) + affine[0]
    out_shape = summed.shape
    per_group = out_shape[3] // NORM_GROUPS
    pixel_count = out_shape[1] * out_shape[2] * per_group
    totals = jnp.stack([jnp.sum(summed, axis=(1, 2)), jnp.sum(jnp.square(summed), axis=(1, 2))])
    totals = jnp.sum(totals.reshape(2, out_shape[0], NORM_GROUPS, per_group), axis=3)
    grp_mean = totals[0] / pixel_count
    grp_var = jnp.maximum(totals[1] / pixel_count - jnp.square(grp_mean), 0.0)
    inv_std = lax.rsqrt(grp_var + NORM_EPS)
    chan_scale = jnp.repeat(inv_std, per_group, axis=1) * affine[1]
    chan_shift = affine[2] - jnp.repeat(grp_mean * inv_std, per_group, axis=1) * affine[1]
    return jax.nn.relu(summed * chan_scale[:, None, None, :] + chan_shift[:, None, None, :]).astype(jnp.bfloat16)


def solution(mesh):
    act_spec = P("batch", "h", "w")

    def local_forward(tile, *params):
        current = lax.all_to_all(tile, "h", 0, 1, tiled=True)
        current = lax.all_to_all(current, "w", 0, 2, tiled=True)
        for stage in range(3):
            down_w, down_v, refine_w, refine_v = params[4 * stage:4 * stage + 4]
            current = conv_norm(current, down_w, down_v, 2)
            current = conv_norm(current, refine_w, refine_v, 1)
        current = lax.all_to_all(current, "w", 2, 0, tiled=True)
        return lax.all_to_all(current, "h", 1, 0, tiled=True)

    return jax.shard_map(local_forward, mesh=mesh, in_specs=(act_spec,) + (P(),) * 12, out_specs=act_spec, check_vma=False)
```

time: 1000 us -> 418 us (0.42)
  waiting for transfers between devices: 484 us -> 21.9 us
  blocking collectives: 282 us -> 104 us
  matrix products: 108 us -> 210 us
  other arithmetic: 58.2 us -> 5.58 us
  local copies, waits for them, and re-layouts: 16.8 us -> 58.9 us
  starting transfers between devices: 41.9 us -> 11.8 us
    ppermute x18 -> x0, waiting for transfers between devices: 484 us -> none  [shift_in(): return lax.ppermute(piece, axis_name, send_pairs)]
    psum x6 -> x0, blocking collectives: 282 us -> none  [conv_norm(): totals = lax.psum(part_sums, ('h', 'w'))]
    all_to_all x0 -> x2, blocking collectives: none -> 104 us  [the longest x1 54.7 us: local_forward(): return lax.all_to_all(current, 'h', 1, 0, tiled=True)]
    conv_general_dilated x6, matrix products: 108 us -> 210 us  [conv_norm(): lax.conv_general_dilated(inputs, kernel, (stride, stride), pads, dimensio...]
    all_to_all x0 -> x6, local copies, waits for them, and re-layouts: none -> 49.5 us  [the longest x2 40.4 us: local_forward(): current = lax.all_to_all(current, 'w', 0, 2, tiled=True)]
    convert_element_type x6 -> x1, other arithmetic: 52.6 us -> 4.89 us  [conv_norm(): jax.nn.relu(summed * chan_scale[:, None, None, :] + chan_shift[:, None, N...]
    ppermute x18 -> x0, starting transfers between devices: 41.9 us -> none  [shift_in(): return lax.ppermute(piece, axis_name, send_pairs)]
    all_to_all x0 -> x2, waiting for transfers between devices: none -> 21.9 us  [the longest x1 14 us: local_forward(): current = lax.all_to_all(tile, 'h', 0, 1, tiled=True)]
  transfers between devices with their start and end apart: 18 -> 2, of which waited for: 15 -> 2; matrix products, arithmetic and copies ran while one was open for 0% -> 2% of each run, Pallas kernels for 0% -> 0%
where the time goes in v1:
time: 418 us; the launch traced here: 412 us
  matrix products  210 us (50%)
  blocking collectives  104 us (25%)
  local copies, waits for them, and re-layouts  58.9 us (14%)
  waiting for transfers between devices  21.9 us (5%)
  starting transfers between devices  11.8 us (3%)
  other arithmetic  5.58 us (1%)
    conv_general_dilated x6, matrix products, conv_norm(): lax.conv_general_dilated(inputs, kernel, (stride, stride), pads, dimensio...  210 us
    all_to_all x1, blocking collectives, local_forward(): return lax.all_to_all(current, 'h', 1, 0, tiled=True)  54.7 us
    all_to_all x1, blocking collectives, local_forward(): current = lax.all_to_all(current, 'w', 2, 0, tiled=True)  49.1 us
    all_to_all x2, local copies, waits for them, and re-layouts, local_forward(): current = lax.all_to_all(current, 'w', 0, 2, tiled=True)  40.4 us
    all_to_all x1, waiting for transfers between devices, local_forward(): current = lax.all_to_all(tile, 'h', 0, 1, tiled=True)  14 us
  transfers between devices with their start and end apart: 2, of which 2 were waited for; matrix products, arithmetic and copies ran while one was open for 2% of the time, Pallas kernels for 0%

profile of v1, /device:TPU:97, one launch (start us, length us, event | category | flops | bytes accessed | tf_op | source)
XLA Modules:
  0.0 412.5 jit_solution(11017821429355455347)
XLA Ops:
  0.0 6.1 %all-to-all-start = ((bf16[256,256,8,1]{1,2,3,0:T(8,128)(2,1)}), bf16[256,256,8,1]{1,2,3,0:T(8,128)(2,1)S(1)}, u32[]{:S(2)}, u32[]{:S(2)}) async-start(bf16[256,256,8,1]{1,2,3,0:T(8,128)(2,1)} %param.13), calls=%async_computation | async-start | bytes 2097152 | tf_op jit(solution)/shard_map/all_to_all | solution.py:30
  6.2 0.8 slice_bitcast_fusion.10
  6.9 14.0 %all-to-all-done = bf16[256,256,8,1]{1,2,3,0:T(8,128)(2,1)S(1)} async-done(((bf16[256,256,8,1]{1,2,3,0:T(8,128)(2,1)}), bf16[256,256,8,1]{1,2,3,0:T(8,128)(2,1)S(1)}, u32[]{:S(2)}, u32[]{:S(2)}) %all-to-all-start) | async-done | bytes 1048608 | tf_op jit(solution)/shard_map/all_to_all | solution.py:30
  20.9 1.1 copy.39
  22.0 5.6 %all-to-all-start.1 = ((bf16[32,2048,8,1]{1,2,3,0:T(8,128)(2,1)}), bf16[32,2048,8,1]{1,2,3,0:T(8,128)(2,1)S(1)}, u32[]{:S(2)}, u32[]{:S(2)}) async-start(bf16[32,2048,8,1]{1,2,3,0:T(8,128)(2,1)} %bitcast.2), calls=%async_computation.1 | async-start | bytes 2097152 | tf_op jit(solution)/shard_map/all_to_all | solution.py:31
  27.7 1.4 slice_bitcast_fusion.7
  29.0 1.4 fusion.77
  30.4 1.4 fusion.76
  31.8 1.4 slice_bitcast_fusion.1
  33.2 7.9 %all-to-all-done.1 = bf16[32,2048,8,1]{1,2,3,0:T(8,128)(2,1)S(1)} async-done(((bf16[32,2048,8,1]{1,2,3,0:T(8,128)(2,1)}), bf16[32,2048,8,1]{1,2,3,0:T(8,128)(2,1)S(1)}, u32[]{:S(2)}, u32[]{:S(2)}) %all-to-all-start.1) | async-done | bytes 1048608 | tf_op jit(solution)/shard_map/all_to_all | solution.py:31
  41.2 0.1 copy.52
  41.3 40.3 %copy.41 = bf16[8,2048,32,1]{0,3,2,1:T(2,128)(2,1)} copy(bf16[8,2048,32,1]{1,2,0,3:T(8,128)(2,1)S(1)} %bitcast.166) | data formatting | bytes 2097152 | tf_op jit(solution)/shard_map/all_to_all | solution.py:31
  81.6 69.7 %add_reduce_fusion.1 = (f32[8,64]{1,0:T(8,128)S(1)}, f32[8,64]{1,0:T(8,128)S(1)}, f32[8,1024,16,64]{3,0,2,1:T(8,128)}) fusion(f32[64]{0:T(128)S(1)} %get-tuple-element.45, bf16[8,2048,32,1]{0,3,2,1:T(2,128)(2,1)} %copy.41, bf16[3,3,1,64]{3,1,2,0:T(4,128)(2,1)S(1)} %copy-done.19), kind=kOutput, calls=%fused_computation.5 | convolution fusion | flops 181354496 | bytes 34608512 | tf_op jit(solution)/shard_map/conv_general_dilated | solution.py:12
  151.4 0.1 maximum_reduce_fusion
  151.5 0.1 broadcast_in_dim.48
  151.6 0.1 reshape.378
  151.6 0.1 broadcast_in_dim.49
  151.7 0.1 reshape.379
  151.9 57.0 %add_reduce_fusion = (f32[8,64]{1,0:T(8,128)S(1)}, f32[8,64]{1,0:T(8,128)S(1)}, f32[8,1024,16,64]{3,0,2,1:T(8,128)}) fusion(f32[64]{0:T(128)S(1)} %get-tuple-element.42, bf16[3,3,64,64]{3,2,1,0:T(8,128)(2,1)S(1)} %copy-done.17, f32[8,1024,16,64]{3,0,2,1:T(8,128)} %get-tuple-element.59, f32[8,64]{1,0:T(8,128)S(1)} %get-tuple-element.58, ...), kind=kOutput, calls=%fused_computation.4 | convolution fusion | flops 9330491392 | bytes 67191296 | tf_op jit(solution)/shard_map/conv_general_dilated | solution.py:12
  209.0 0.1 maximum_reduce_fusion.1
  209.2 0.1 reshape.380
  209.3 0.1 broadcast_in_dim.51
  209.4 0.1 reshape.381
  209.5 31.3 %add_reduce_fusion.3 = (f32[8,128]{1,0:T(8,128)S(1)}, f32[8,128]{1,0:T(8,128)S(1)}, f32[8,512,8,128]{3,0,2,1:T(8,128)}) fusion(f32[128]{0:T(128)S(1)} %copy-done.14, bf16[3,3,64,128]{3,2,1,0:T(8,128)(2,1)S(1)} %copy-done.18, f32[8,1024,16,64]{3,0,2,1:T(8,128)} %get-tuple-element.60, f32[8,64]{1,0:T(8,128)S(1)} %get-tuple-element.56, ...), kind=kOutput, calls=%fused_computation.17 | convolution fusion | flops 4686215168 | bytes 50492160 | tf_op jit(solution)/shard_map/conv_general_dilated | solution.py:12
  241.0 0.1 maximum_reduce_fusion.2
  241.2 0.1 reshape.382
  241.3 0.1 broadcast_in_dim.53
  241.3 0.1 reshape.383
  241.5 24.6 %add_reduce_fusion.2 = (f32[8,128]{1,0:T(8,128)S(1)}, f32[8,128]{1,0:T(8,128)S(1)}, f32[8,512,8,128]{3,0,2,1:T(8,128)}) fusion(f32[128]{0:T(128)S(1)} %copy-done.13, bf16[3,3,128,128]{3,2,1,0:T(8,128)(2,1)S(1)} %copy-done.16, f32[8,512,8,128]{3,0,2,1:T(8,128)} %get-tuple-element.61, f32[8,128]{1,0:T(8,128)S(1)} %get-tuple-element.54, ...), kind=kOutput, calls=%fused_computation.16 | convolution fusion | flops 8884582400 | bytes 33866752 | tf_op jit(solution)/shard_map/conv_general_dilated | solution.py:12
  266.3 0.1 maximum_reduce_fusion.3
  266.5 0.1 reshape.384
  266.5 0.1 broadcast_in_dim.55
  266.6 0.1 reshape.385
  266.8 12.2 %add_reduce_fusion.5 = (f32[8,256]{1,0:T(8,128)S(1)}, f32[8,256]{1,0:T(8,128)S(1)}, f32[8,256,4,256]{3,0,2,1:T(8,128)}) fusion(f32[256]{0:T(256)S(1)} %bitcast.175, bf16[3,3,128,256]{3,2,1,0:T(8,128)(2,1)S(1)} %copy-done.15, f32[8,512,8,128]{3,0,2,1:T(8,128)} %get-tuple-element.62, f32[8,128]{1,0:T(8,128)S(1)} %get-tuple-element.52, ...), kind=kOutput, calls=%fused_computation.33 | convolution fusion | flops 4452773888 | bytes 25781760 | tf_op jit(solution)/shard_map/conv_general_dilated | solution.py:12
  279.2 0.1 maximum_reduce_fusion.4
  279.3 0.1 reshape.386
  279.5 0.1 reshape.387
  279.6 15.1 %add_reduce_fusion.4 = (f32[8,256]{1,0:T(8,128)S(1)}, f32[8,256]{1,0:T(8,128)S(1)}, f32[8,256,4,256]{3,0,2,1:T(8,128)}) fusion(f32[256]{0:T(256)S(1)} %bitcast.169, bf16[3,3,256,256]{3,2,1,0:T(8,128)(2,1)S(1)} %copy-done, f32[8,256,4,256]{3,0,2,1:T(8,128)} %get-tuple-element.63, f32[8,256]{1,0:T(8,128)S(1)} %get-tuple-element.50, ...), kind=kOutput, calls=%fused_computation.32 | convolution fusion | flops 8050962432 | bytes 17991680 | tf_op jit(solution)/shard_map/conv_general_dilated | solution.py:12
  294.9 0.1 maximum_reduce_fusion.5
  295.1 0.1 reshape.388
  295.2 0.1 reshape.389
  295.3 4.9 %maximum_convert_fusion.8 = bf16[8,256,4,256]{3,0,2,1:T(8,128)(2,1)S(1)} fusion(f32[8,256,4,256]{3,0,2,1:T(8,128)} %get-tuple-element.64, f32[8,256]{1,0:T(8,128)S(1)} %get-tuple-element.48, f32[8,256]{1,0:T(8,128)S(1)} %get-tuple-element.47, f32[256]{0:T(256)S(1)} %bitcast.170), kind=kLoop, calls=%fused_computation.20 | loop fusion | flops 10485760 | bytes 12600320 | tf_op jit(solution)/shard_map/convert_element_type | solution.py:23
  300.2 0.3 copy.43
  300.5 49.1 %all_to_all.72 = bf16[8,256,4,256]{3,0,1,2:T(8,128)(2,1)S(1)} all-to-all(bf16[8,256,4,256]{3,0,1,2:T(8,128)(2,1)S(1)} %copy.43), channel_id=1, replica_groups=mesh['batch'=1,'w'=4,'h'=8] {'w'}, dimensions={2} | all-to-all | bytes 8388608 | tf_op jit(solution)/shard_map/all_to_all | solution.py:36
  349.6 1.0 copy.44
  350.6 2.4 copy.45
  353.0 54.7 %all_to_all.73 = bf16[32,256,1,256]{3,0,2,1:T(8,128)(2,1)S(1)} all-to-all(bf16[32,256,1,256]{3,0,2,1:T(8,128)(2,1)S(1)} %copy.45), channel_id=1, replica_groups=mesh['batch'=1,'w'=4,'h'=8] {'h'}, dimensions={1} | all-to-all | bytes 8388608 | tf_op jit(solution)/shard_map/all_to_all | solution.py:37
  407.7 4.6 %copy.46 = bf16[8,32,32,1,256]{4,2,1,0,3:T(8,128)(2,1)} copy(bf16[8,32,32,1,256]{4,1,2,0,3:T(8,128)(2,1)S(1)} %bitcast.165) | data formatting | bytes 8388608 | tf_op jit(solution)/shard_map/all_to_all | solution.py:37
  (71 shorter events, 1.6 us)
Async XLA Ops:
  0.0 279.6 %copy-start = (bf16[3,3,256,256]{3,2,1,0:T(8,128)(2,1)S(1)}, bf16[3,3,256,256]{3,2,1,0:T(8,128)(2,1)}, u32[]{:S(2)}) copy-start(bf16[3,3,256,256]{3,2,1,0:T(8,128)(2,1)} %param.24) | copy-start | bytes 3538948
  0.0 20.9 %all-to-all-start = ((bf16[256,256,8,1]{1,2,3,0:T(8,128)(2,1)}), bf16[256,256,8,1]{1,2,3,0:T(8,128)(2,1)S(1)}, u32[]{:S(2)}, u32[]{:S(2)}) async-start(bf16[256,256,8,1]{1,2,3,0:T(8,128)(2,1)} %param.13), calls=%async_computation | async-start | bytes 2097152 | tf_op jit(solution)/shard_map/all_to_all | solution.py:30
  22.0 19.2 %all-to-all-start.1 = ((bf16[32,2048,8,1]{1,2,3,0:T(8,128)(2,1)}), bf16[32,2048,8,1]{1,2,3,0:T(8,128)(2,1)S(1)}, u32[]{:S(2)}, u32[]{:S(2)}) async-start(bf16[32,2048,8,1]{1,2,3,0:T(8,128)(2,1)} %bitcast.2), calls=%async_computation.1 | async-start | bytes 2097152 | tf_op jit(solution)/shard_map/all_to_all | solution.py:31
  41.3 40.3 %copy-start.19 = (bf16[3,3,1,64]{3,1,2,0:T(4,128)(2,1)S(1)}, bf16[3,3,1,64]{3,1,2,0:T(4,128)(2,1)}, u32[]{:S(2)}) copy-start(bf16[3,3,1,64]{3,1,2,0:T(4,128)(2,1)} %param.14) | copy-start | bytes 3460
  81.5 70.3 %copy-start.17 = (bf16[3,3,64,64]{3,2,1,0:T(8,128)(2,1)S(1)}, bf16[3,3,64,64]{3,2,1,0:T(8,128)(2,1)}, u32[]{:S(2)}) copy-start(bf16[3,3,64,64]{3,2,1,0:T(8,128)(2,1)} %param.16) | copy-start | bytes 221188
  151.8 57.6 %copy-start.10 = (f32[64]{0:T(128)S(1)}, f32[64]{0:T(128)}, u32[]{:S(2)}) copy-start(f32[64]{0:T(128)} %get-tuple-element.41) | copy-start | bytes 772
  151.8 57.6 %copy-start.11 = (f32[64]{0:T(128)S(1)}, f32[64]{0:T(128)}, u32[]{:S(2)}) copy-start(f32[64]{0:T(128)} %get-tuple-element.43) | copy-start | bytes 772
  151.8 57.7 %copy-start.14 = (f32[128]{0:T(128)S(1)}, f32[128]{0:T(128)}, u32[]{:S(2)}) copy-start(f32[128]{0:T(128)} %get-tuple-element.66) | copy-start | bytes 1540
  151.8 57.7 %copy-start.18 = (bf16[3,3,64,128]{3,2,1,0:T(8,128)(2,1)S(1)}, bf16[3,3,64,128]{3,2,1,0:T(8,128)(2,1)}, u32[]{:S(2)}) copy-start(bf16[3,3,64,128]{3,2,1,0:T(8,128)(2,1)} %param.18) | copy-start | bytes 442372
  209.5 31.9 %copy-start.8 = (f32[128]{0:T(128)S(1)}, f32[128]{0:T(128)}, u32[]{:S(2)}) copy-start(f32[128]{0:T(128)} %get-tuple-element.65) | copy-start | bytes 1540
  209.5 31.9 %copy-start.9 = (f32[128]{0:T(128)S(1)}, f32[128]{0:T(128)}, u32[]{:S(2)}) copy-start(f32[128]{0:T(128)} %get-tuple-element.67) | copy-start | bytes 1540
  209.5 31.9 %copy-start.13 = (f32[128]{0:T(128)S(1)}, f32[128]{0:T(128)}, u32[]{:S(2)}) copy-start(f32[128]{0:T(128)} %get-tuple-element.36) | copy-start | bytes 1540
  209.5 31.9 %copy-start.16 = (bf16[3,3,128,128]{3,2,1,0:T(8,128)(2,1)S(1)}, bf16[3,3,128,128]{3,2,1,0:T(8,128)(2,1)}, u32[]{:S(2)}) copy-start(bf16[3,3,128,128]{3,2,1,0:T(8,128)(2,1)} %param.20) | copy-start | bytes 884740
  241.5 25.2 %copy-start.6 = (f32[128]{0:T(128)S(1)}, f32[128]{0:T(128)}, u32[]{:S(2)}) copy-start(f32[128]{0:T(128)} %get-tuple-element.35) | copy-start | bytes 1540
  241.5 25.2 %copy-start.7 = (f32[128]{0:T(128)S(1)}, f32[128]{0:T(128)}, u32[]{:S(2)}) copy-start(f32[128]{0:T(128)} %get-tuple-element.37) | copy-start | bytes 1540
  241.5 25.2 %copy-start.12 = (f32[1,256]{1,0:T(1,128)S(1)}, f32[1,256]{1,0:T(1,128)}, u32[]{:S(2)}) copy-start(f32[1,256]{1,0:T(1,128)} %get-tuple-element.33) | copy-start | bytes 3076
  241.5 25.2 %copy-start.15 = (bf16[3,3,128,256]{3,2,1,0:T(8,128)(2,1)S(1)}, bf16[3,3,128,256]{3,2,1,0:T(8,128)(2,1)}, u32[]{:S(2)}) copy-start(bf16[3,3,128,256]{3,2,1,0:T(8,128)(2,1)} %param.22) | copy-start | bytes 1769476
  266.7 12.8 %copy-start.4 = (f32[1,256]{1,0:T(1,128)S(1)}, f32[1,256]{1,0:T(1,128)}, u32[]{:S(2)}) copy-start(f32[1,256]{1,0:T(1,128)} %get-tuple-element.32) | copy-start | bytes 3076
  266.7 12.8 %copy-start.5 = (f32[1,256]{1,0:T(1,128)S(1)}, f32[1,256]{1,0:T(1,128)}, u32[]{:S(2)}) copy-start(f32[1,256]{1,0:T(1,128)} %get-tuple-element.34) | copy-start | bytes 3076
  266.8 12.9 %copy-start.1 = (f32[1,256]{1,0:T(1,128)S(1)}, f32[1,256]{1,0:T(1,128)}, u32[]{:S(2)}) copy-start(f32[1,256]{1,0:T(1,128)} %get-tuple-element.30) | copy-start | bytes 3076
  279.6 15.7 %copy-start.2 = (f32[1,256]{1,0:T(1,128)S(1)}, f32[1,256]{1,0:T(1,128)}, u32[]{:S(2)}) copy-start(f32[1,256]{1,0:T(1,128)} %get-tuple-element.29) | copy-start | bytes 3076
  279.6 15.7 %copy-start.3 = (f32[1,256]{1,0:T(1,128)S(1)}, f32[1,256]{1,0:T(1,128)}, u32[]{:S(2)}) copy-start(f32[1,256]{1,0:T(1,128)} %get-tuple-element.31) | copy-start | bytes 3076

commit v2 on v1

v2 whole, which is shorter than its diff:
```python
import functools

import jax
import jax.numpy as jnp
from jax import lax
from jax.experimental import pallas as pl
from jax.experimental.pallas import tpu as pltpu
from jax.sharding import PartitionSpec as P

NORM_GROUPS = 8
NORM_EPS = 1e-5
F32 = jnp.float32
BF16 = jnp.bfloat16
LANES = 128
STRIPS = 16


def iota(shape, dim):
    return lax.broadcasted_iota(jnp.int32, shape, dim)


def div(value, by):
    return lax.div(value, jnp.int32(by))


def rem(value, by):
    return lax.rem(value, jnp.int32(by))


def blend(pieces, rows, cols):
    return jnp.concatenate([jnp.zeros((rows, cols), BF16) if piece is None else piece for piece in pieces], axis=1)


def tap(ref, depth, row, col):
    if 0 <= row < 3 and 0 <= col < 3:
        return ref[pl.ds((3 * row + col) * depth, depth), :]
    return None


def build_weights(w1_ref, r1_ref, d2_ref, r2_ref, m1, m2, m3, m4, cols):
    taps = w1_ref[...].astype(F32)
    taps = jnp.concatenate([taps] * 4, axis=1)
    shape = (2 * LANES, 2 * LANES)
    k, n = iota(shape, 0), iota(shape, 1)
    kk = rem(k, LANES)
    row = 4 * (div(k, LANES) - 1) + rem(div(kk, 8), 4)
    col = 8 * div(kk, 32) + rem(kk, 8)
    d_row = row - 2 * div(n, LANES) + 1
    half = rem(div(n, 64), 2)
    row_ok = (d_row >= 0) & (d_row < 3)

    def one_block(block, _):
        col_out = 2 * block - 1 + half
        d_col = col - 2 * col_out + 1
        good = row_ok & (d_col >= 0) & (d_col < 3) & (col_out >= 0) & (col_out < cols // 2)
        code = jnp.where(good, 3 * d_row + d_col, -1)
        total = jnp.zeros(shape, F32)
        for index in range(9):
            total = jnp.where(code == index, taps[index:index + 1], total)
        m1[block] = total.astype(BF16)
        return 0

    lax.fori_loop(0, m1.shape[0], one_block, 0)
    for t in range(4):
        for q in range(4):
            m2[pl.ds((4 * t + q) * 64, 64), :] = blend([tap(r1_ref, 64, t - r, q - g) for r in range(2) for g in range(2)], 64, 64)
    for t in range(3):
        for q in range(6):
            m3[pl.ds((6 * t + q) * 64, 64), :] = blend([tap(d2_ref, 64, t, q - 1 - 2 * g) for g in range(2)], 64, LANES)
    for t in range(3):
        for q in range(4):
            m4[pl.ds((4 * t + q) * LANES, LANES), :] = blend([tap(r2_ref, LANES, t, q - g) for g in range(2)], LANES, LANES)


def group_matrix(period, group):
    shape = (LANES, LANES)
    return jnp.where(div(rem(iota(shape, 0), period), group) == div(rem(iota(shape, 1), period), group), 1.0, 0.0).astype(F32)


def down_strip(row):
    return jnp.where(iota(row.shape, 0) == 0, 0.0, pltpu.roll(row, 1, 0))


def up_strip(row):
    return jnp.where(iota(row.shape, 0) == STRIPS - 1, 0.0, pltpu.roll(row, STRIPS - 1, 0))


def coefficients(sums, squares, folds, gamma, beta, count):
    both = jnp.concatenate([sums, squares], axis=0)
    both = jnp.dot(both, folds, preferred_element_type=F32, precision=lax.Precision.HIGHEST)
    total = jnp.sum(both[:STRIPS], axis=0, keepdims=True)
    total_sq = jnp.sum(both[STRIPS:], axis=0, keepdims=True)
    mean = total / count
    var = jnp.maximum(total_sq / count - jnp.square(mean), 0.0)
    inv = lax.rsqrt(var + NORM_EPS)
    scale = inv * gamma
    return scale, beta - mean * scale


class Stream:
    def __init__(self, mats, affines, acc, x, y1, z1, y2, z2, y3, out, cols):
        self.mats, self.affines = mats, affines
        self.acc, self.x, self.y1, self.z1, self.y2, self.z2, self.y3, self.out = acc, x, y1, z1, y2, z2, y3, out
        self.cols = cols
        self.q = x.shape[0] - 1
        self.r2 = y2.shape[1] - 2
        self.r3 = y3.shape[2] - 2
        self.sums = None
        self.squares = None

    def lhs(self, parts):
        parts = [part.reshape(part.shape[0] * STRIPS, LANES) for part in parts]
        return jnp.concatenate(parts, axis=1)

    def finish(self, summed, bias, first, second):
        rows = summed.shape[0]
        summed = summed + bias
        cube = summed.reshape(rows // STRIPS, STRIPS, 2 * LANES)
        sums, squares = jnp.sum(cube, axis=0), jnp.sum(cube * cube, axis=0)
        self.sums = sums if self.sums is None else self.sums + sums
        self.squares = squares if self.squares is None else self.squares + squares
        self.acc[first, 0:rows] = summed[:, :LANES]
        self.acc[second, 0:rows] = summed[:, LANES:]

    def two(self, row):
        return jnp.concatenate([row, row], axis=1)

    def conv1(self):
        affine = self.affines[0]
        lane = iota((1, LANES), 1)
        blocks = self.mats[0].shape[0]
        bias = self.two(affine[0:1])

        def piece(block):
            own = bias
            if block == 0:
                own = self.two(jnp.where(lane < 64, 0.0, affine[0:1]))
            elif block == blocks - 1:
                own = self.two(jnp.where(lane < 64, affine[0:1], 0.0))
            left = self.lhs([self.x[0:self.q], self.x[1:self.q + 1]])
            self.finish(jnp.dot(left, self.mats[0][block], preferred_element_type=F32), own, 2 * block, 2 * block + 1)

        return [functools.partial(piece, block) for block in range(blocks)]

    def conv2(self):
        bias, q = self.two(self.affines[1][0:1]), self.q

        def piece(block):
            parts = []
            for parity, start in ((1, 0), (0, 1), (1, 1), (0, 2)):
                for near in range(2):
                    parts.append(self.y1[block + near, parity, start:start + q])
            self.finish(jnp.dot(self.lhs(parts), self.mats[1][...], preferred_element_type=F32), bias, 2 * block, 2 * block + 1)

        return [functools.partial(piece, block) for block in range(self.cols // 4)]

    def conv3(self):
        bias, q = self.two(self.affines[2][0:1]), self.q

        def piece(block):
            parts = []
            for parity, start in ((1, 0), (0, 1), (1, 1)):
                for near in range(3):
                    parts.append(self.z1[2 * block + near, parity, start:start + q])
            self.finish(jnp.dot(self.lhs(parts), self.mats[2][...], preferred_element_type=F32), bias, 2 * block, 2 * block + 1)

        return [functools.partial(piece, block) for block in range(self.cols // 8)]

    def conv4(self):
        bias = self.two(self.affines[3][0:1])

        def piece(block):
            parts = []
            for start in range(3):
                for near in range(4):
                    parts.append(self.y2[2 * block + near, start:start + self.r2])
            self.finish(jnp.dot(self.lhs(parts), self.mats[3][...], preferred_element_type=F32), bias, 2 * block, 2 * block + 1)

        return [functools.partial(piece, block) for block in range(self.cols // 8)]

    def conv5(self):
        bias = self.affines[4][0:1]

        def piece(col):
            parts = []
            for parity, start in ((1, 0), (0, 1), (1, 1)):
                for near in range(3):
                    parts.append(self.z2[2 * col + near, parity, start:start + self.r3])
            self.finish(jnp.dot(self.lhs(parts), self.mats[4][...], preferred_element_type=F32), bias, 2 * col, 2 * col + 1)

        return [functools.partial(piece, col) for col in range(self.cols // 8)]

    def conv6(self):
        bias = self.affines[5][0:1]

        def piece(col):
            parts = []
            for start in range(3):
                for near in range(3):
                    for half in range(2):
                        parts.append(self.y3[col + near, half, start:start + self.r3])
            self.finish(jnp.dot(self.lhs(parts), self.mats[5][...], preferred_element_type=F32), bias, 2 * col, 2 * col + 1)

        return [functools.partial(piece, col) for col in range(self.cols // 8)]

    def stats(self, layer):
        affine = self.affines[layer]
        period, group = ((64, 8), (LANES, 16), (LANES, 32))[layer // 2]
        folds = group_matrix(period, group)
        height = 1
        rows = (2 * self.q, self.r2, self.r3)[layer // 2]
        width = self.cols >> (layer // 2 + 1)
        count = float(height * rows * STRIPS * width * group)
        sums, squares = self.sums, self.squares
        self.sums = self.squares = None
        if layer < 4:
            sums, squares = sums[:, :LANES] + sums[:, LANES:], squares[:, :LANES] + squares[:, LANES:]
            self.scale, self.shift = coefficients(sums, squares, folds, affine[1:2], affine[2:3], count)
        else:
            pairs = [coefficients(sums[:, lo:lo + LANES], squares[:, lo:lo + LANES], folds, affine[1:2, lo:lo + LANES], affine[2:3, lo:lo + LANES], count) for lo in (0, LANES)]
            self.scale, self.shift = [pair[0] for pair in pairs], [pair[1] for pair in pairs]

    def apply(self, block, rows, scale, shift):
        cube = jnp.maximum(self.acc[block, 0:rows * STRIPS] * scale + shift, 0.0)
        return cube.reshape(rows, STRIPS, LANES)

    def norm1(self):
        lane, q = iota((1, LANES), 1), self.q
        blocks = self.mats[0].shape[0]

        def piece(block, parity):
            scale, shift = self.scale, self.shift
            if block == 0:
                scale, shift = jnp.where(lane < 64, 0.0, scale), jnp.where(lane < 64, 0.0, shift)
            elif block == blocks - 1:
                scale, shift = jnp.where(lane < 64, scale, 0.0), jnp.where(lane < 64, shift, 0.0)
            cube = self.apply(2 * block + parity, q, scale, shift)
            self.y1[block, parity, 1:q + 1] = cube.astype(BF16)
            if parity:
                self.y1[block, 1, 0] = down_strip(cube[q - 1]).astype(BF16)
            else:
                self.y1[block, 0, q + 1] = up_strip(cube[0]).astype(BF16)

        return [functools.partial(piece, block, parity) for block in range(blocks) for parity in range(2)]

    def norm2(self):
        q = self.q

        def piece(block, parity):
            cube = self.apply(2 * block + parity, q, self.scale, self.shift)
            self.z1[block + 1, parity, 1:q + 1] = cube.astype(BF16)
            if parity:
                self.z1[block + 1, 1, 0] = down_strip(cube[q - 1]).astype(BF16)

        return [functools.partial(piece, block, parity) for block in range(self.cols // 4) for parity in range(2)]

    def norm3(self):
        rows = self.r2

        def piece(col):
            cube = self.apply(col, rows, self.scale, self.shift)
            self.y2[col + 1, 1:rows + 1] = cube.astype(BF16)
            self.y2[col + 1, 0] = down_strip(cube[rows - 1]).astype(BF16)
            self.y2[col + 1, rows + 1] = up_strip(cube[0]).astype(BF16)

        return [functools.partial(piece, col) for col in range(self.cols // 4)]

    def norm4(self):
        rows = self.r3

        def piece(col):
            cube = self.apply(col, 2 * rows, self.scale, self.shift).reshape(rows, 2, STRIPS, LANES)
            self.z2[col + 1, 0, 1:rows + 1] = cube[:, 0].astype(BF16)
            self.z2[col + 1, 1, 1:rows + 1] = cube[:, 1].astype(BF16)
            self.z2[col + 1, 1, 0] = down_strip(cube[rows - 1, 1]).astype(BF16)

        return [functools.partial(piece, col) for col in range(self.cols // 4)]

    def norm5(self):
        rows = self.r3

        def piece(col, half):
            cube = self.apply(2 * col + half, rows, self.scale[half], self.shift[half])
            self.y3[col + 1, half, 1:rows + 1] = cube.astype(BF16)
            self.y3[col + 1, half, 0] = down_strip(cube[rows - 1]).astype(BF16)
            self.y3[col + 1, half, rows + 1] = up_strip(cube[0]).astype(BF16)

        return [functools.partial(piece, col, half) for col in range(self.cols // 8) for half in range(2)]

    def norm6(self):
        rows = self.r3
        row_parts = self.out.shape[0] // (self.cols // 8)
        per = STRIPS // row_parts

        def piece(col, half):
            for strip in range(STRIPS):
                part = self.acc[2 * col + half, pl.ds(strip, rows, stride=STRIPS), :]
                part = jnp.maximum(part * self.scale[half] + self.shift[half], 0.0)
                self.out[col * row_parts + strip // per, pl.ds((strip % per) * rows, rows), pl.ds(half * LANES, LANES)] = part.astype(BF16)

        return [functools.partial(piece, col, half) for col in range(self.cols // 8) for half in range(2)]

    def convs(self):
        return [self.conv1, self.conv2, self.conv3, self.conv4, self.conv5, self.conv6]

    def norms(self):
        return [self.norm1, self.norm2, self.norm3, self.norm4, self.norm5, self.norm6]


def load_image(stage_ref, image, x):
    quads = x.shape[0] - 1
    for quad in range(quads):
        row = stage_ref[image, pl.ds(quad, STRIPS, stride=quads), :]
        x[quad + 1] = row.astype(BF16)
        if quad == quads - 1:
            x[0] = down_strip(row).astype(BF16)


def zero_borders(z1, y2, z2, y3):
    z1[0] = jnp.zeros(z1.shape[1:], BF16)
    y2[0] = jnp.zeros(y2.shape[1:], BF16)
    y2[y2.shape[0] - 1] = jnp.zeros(y2.shape[1:], BF16)
    z2[0] = jnp.zeros(z2.shape[1:], BF16)
    y3[0] = jnp.zeros(y3.shape[1:], BF16)
    y3[y3.shape[0] - 1] = jnp.zeros(y3.shape[1:], BF16)


MESH = pl.DeviceIdType.MESH


def pack(x_ref, perm, packed):
    pairs, _, tile_cols, rows = x_ref.shape
    quads = rows // 4
    shape = (2 * rows, 4 * 2 * quads)
    k, n = iota(shape, 0), iota(shape, 1)
    row, image = rem(k, rows), div(k, rows)
    hit = (rem(row, 4) == div(n, 2 * quads)) & (div(row, 4) == rem(n, quads)) & (image == rem(div(n, quads), 2))
    perm[...] = jnp.where(hit, 1.0, 0.0).astype(BF16)
    step = 32

    def one(chunk, _):
        at = pl.ds(chunk * step, step)
        left = jnp.concatenate([x_ref[at, m].astype(F32).reshape(step * tile_cols, rows) for m in range(2)], axis=1).astype(BF16)
        moved = jnp.dot(left, perm[...], preferred_element_type=F32).reshape(step, tile_cols, shape[1])
        moved = jnp.concatenate([moved[:, :, t * LANES:(t + 1) * LANES] for t in range(4)], axis=1)
        packed[at] = moved.astype(BF16)
        return 0

    lax.fori_loop(0, pairs // step, one, 0)


def kernel(rows_n, cols_n, x_ref, w1, v1, r1, u1, d2, v2, r2, u2, d3, v3, r3, u3, o_ref, perm, packed, landed, staged,
           m1, m2, m3, m4, acc, x, y1, z1, y2, z2, y3, out, in_send, in_recv, out_send, out_recv, out_own):
    devices = rows_n * cols_n
    my_row, my_col = lax.axis_index("h"), lax.axis_index("w")
    me = my_col * rows_n + my_row
    pair_n = landed.shape[0]
    cols = cols_n * x_ref.shape[2]

    def place(offset):
        other = lax.rem(me + offset, devices)
        return other, {"h": lax.rem(other, rows_n), "w": lax.div(other, rows_n)}

    barrier = pltpu.get_barrier_semaphore()

    def greet(offset, _):
        pl.semaphore_signal(barrier, inc=1, device_id=place(offset)[1], device_id_type=MESH)
        return 0

    lax.fori_loop(1, devices, greet, 0)
    pack(x_ref, perm, packed)
    pl.semaphore_wait(barrier, devices - 1)

    def send_pair(pair, _):
        pltpu.make_async_copy(packed.at[me * pair_n + pair], landed.at[pair, my_row, my_col], in_recv.at[pair]).start()

        def send(offset, _):
            other, coords = place(offset)
            pltpu.make_async_remote_copy(
                src_ref=packed.at[other * pair_n + pair], dst_ref=landed.at[pair, my_row, my_col], send_sem=in_send,
                recv_sem=in_recv.at[pair], device_id=coords, device_id_type=MESH).start()
            return 0

        lax.fori_loop(1, devices, send, 0)
        return 0

    lax.fori_loop(0, pair_n, send_pair, 0)
    build_weights(w1, r1, d2, r2, m1, m2, m3, m4, cols)
    zero_borders(z1, y2, z2, y3)

    def two(ref):
        row = ref[...]
        return jnp.concatenate([row, row], axis=1)

    affines = [two(v1), two(u1), v2[...], u2[...], v3[...], u3[...]]
    mats = [m1, m2, m3, m4, d3, r3]
    quads = staged.shape[1] // rows_n

    def sent(slot):
        part = out.at[slot, pl.ds(0, devices - 1)]
        pltpu.make_async_copy(part, part, out_send.at[slot]).wait()
        pltpu.make_async_copy(out.at[slot, 0], out.at[slot, 0], out_own.at[slot]).wait()

    def one_pair(pair, _):
        pltpu.make_async_copy(landed.at[pair], landed.at[pair], in_recv.at[pair]).wait()
        for row in range(rows_n):
            turned = jnp.transpose(landed[pair, row].astype(F32).reshape(LANES, LANES))
            for m in range(2):
                staged[m, pl.ds(row * quads, quads)] = turned[m * quads:(m + 1) * quads]

        def one_image(m, _):
            load_image(staged, m, x)
            stream = Stream(mats, affines, acc, x, y1, z1, y2, z2, y3, out.at[m], cols)
            for layer in range(6):
                for piece in stream.convs()[layer]():
                    piece()
                stream.stats(layer)
                if layer == 5:
                    pl.when(pair > 0)(lambda: sent(m))
                for piece in stream.norms()[layer]():
                    piece()
            image = (me * pair_n + pair) * 2 + m
            pltpu.make_async_copy(out.at[m, me], o_ref.at[image], out_own.at[m]).start()

            def send(offset, _):
                other, coords = place(offset)
                pltpu.make_async_remote_copy(
                    src_ref=out.at[m, other], dst_ref=o_ref.at[image], send_sem=out_send.at[m], recv_sem=out_recv,
                    device_id=coords, device_id_type=MESH).start()
                return 0

            lax.fori_loop(1, devices, send, 0)
            return 0

        lax.fori_loop(0, 2, one_image, 0)
        return 0

    lax.fori_loop(0, pair_n, one_pair, 0)
    part = packed.at[pl.ds(0, pair_n * (devices - 1))]
    pltpu.make_async_copy(part, part, in_send).wait()
    sent(0)
    sent(1)
    part = o_ref.at[pl.ds(0, 2 * pair_n * (devices - 1))]
    pltpu.make_async_copy(part, part, out_recv).wait()


def solution(mesh):
    rows_n, cols_n = mesh.shape["h"], mesh.shape["w"]
    devices = rows_n * cols_n
    act_spec = P("batch", "h", "w")

    def local_forward(tile, *params):
        images, rows, tile_cols, _ = tile.shape
        cols = cols_n * tile_cols
        pairs = images // 2
        q = rows_n * rows // 4 // STRIPS
        blocks = cols // 4 + 1
        r2, r3 = q, q // 2
        x = jnp.transpose(tile, (0, 3, 2, 1)).reshape(pairs, 2, tile_cols, rows)
        flat = [param.reshape(-1, param.shape[-1]) for param in params]
        scratch = [
            pltpu.VMEM((2 * rows, 2 * rows), BF16),
            pltpu.VMEM((pairs, 4 * tile_cols, LANES), BF16),
            pltpu.VMEM((pairs // devices, rows_n, cols_n, 4 * tile_cols, LANES), BF16),
            pltpu.VMEM((2, q * STRIPS, LANES), F32),
            pltpu.VMEM((blocks, 2 * LANES, 2 * LANES), BF16),
            pltpu.VMEM((16 * 64, 2 * LANES), BF16),
            pltpu.VMEM((18 * 64, 2 * LANES), BF16),
            pltpu.VMEM((12 * LANES, 2 * LANES), BF16),
            pltpu.VMEM((2 * blocks, q * STRIPS, LANES), F32),
            pltpu.VMEM((q + 1, STRIPS, LANES), BF16),
            pltpu.VMEM((blocks, 2, q + 2, STRIPS, LANES), BF16),
            pltpu.VMEM((blocks, 2, q + 1, STRIPS, LANES), BF16),
            pltpu.VMEM((cols // 4 + 2, r2 + 2, STRIPS, LANES), BF16),
            pltpu.VMEM((cols // 4 + 1, 2, r3 + 1, STRIPS, LANES), BF16),
            pltpu.VMEM((cols // 8 + 2, 2, r3 + 2, STRIPS, LANES), BF16),
            pltpu.VMEM((2, devices, r3 * STRIPS // rows_n, 2 * LANES), BF16),
            pltpu.SemaphoreType.DMA,
            pltpu.SemaphoreType.DMA((pairs // devices,)),
            pltpu.SemaphoreType.DMA((2,)),
            pltpu.SemaphoreType.DMA,
            pltpu.SemaphoreType.DMA((2,)),
        ]
        out = pl.pallas_call(
            functools.partial(kernel, rows_n, cols_n),
            out_shape=jax.ShapeDtypeStruct((images, r3 * STRIPS // rows_n, 2 * LANES), BF16),
            in_specs=[pl.BlockSpec(memory_space=pltpu.VMEM)] * 13,
            out_specs=pl.BlockSpec(memory_space=pl.ANY),
            scratch_shapes=scratch,
            name="encoder",
            compiler_params=pltpu.CompilerParams(collective_id=0, has_side_effects=True, vmem_limit_bytes=56 * 1024 * 1024),
        )(x, *flat)
        return out.reshape(images, out.shape[1], 1, 2 * LANES)

    return jax.shard_map(local_forward, mesh=mesh, in_specs=(act_spec,) + (P(),) * 12, out_specs=act_spec, check_vma=False)
```

time: 418 us -> 131 us (0.31); the launches traced: 412 us -> 131 us
  matrix products: 210 us -> 0 us
  Pallas kernels: 0 us -> 125 us
  blocking collectives: 104 us -> 0 us
  local copies, waits for them, and re-layouts: 58.9 us -> 5.93 us
  waiting for transfers between devices: 21.9 us -> 0 us
  starting transfers between devices: 11.8 us -> 0 us
  other arithmetic: 5.58 us -> 0 us
    conv_general_dilated x6 -> x0, matrix products: 210 us -> none  [conv_norm(): lax.conv_general_dilated(inputs, kernel, (stride, stride), pads, dimensio...]
    pallas_call x0 -> x1, Pallas kernels: none -> 125 us  [local_forward(): pl.pallas_call(functools.partial(kernel, rows_n, cols_n), out_shape=jax.S...]
    all_to_all x2 -> x0, blocking collectives: 104 us -> none  [the longest x1 54.7 us: local_forward(): return lax.all_to_all(current, 'h', 1, 0, tiled=True)]
    all_to_all x6 -> x0, local copies, waits for them, and re-layouts: 49.5 us -> none  [the longest x2 40.4 us: local_forward(): current = lax.all_to_all(current, 'w', 0, 2, tiled=True)]
    all_to_all x2 -> x0, waiting for transfers between devices: 21.9 us -> none  [the longest x1 14 us: local_forward(): current = lax.all_to_all(tile, 'h', 0, 1, tiled=True)]
    all_to_all x2 -> x0, starting transfers between devices: 11.8 us -> none  [the longest x1 6.15 us: local_forward(): current = lax.all_to_all(tile, 'h', 0, 1, tiled=True)]
    convert_element_type x1 -> x0, other arithmetic: 4.89 us -> none  [conv_norm(): jax.nn.relu(summed * chan_scale[:, None, None, :] + chan_shift[:, None, N...]
    unnamed x40 -> x1, local copies, waits for them, and re-layouts: 0.11 us -> 4.64 us
  transfers between devices with their start and end apart: 2 -> 0, of which waited for: 2 -> 0; matrix products, arithmetic and copies ran while one was open for 2% -> 0% of each run, Pallas kernels for 0% -> 0%
where the time goes in v2:
time: 131 us
  Pallas kernels  125 us (95%)
  local copies, waits for them, and re-layouts  5.93 us (5%)
    pallas_call x1, Pallas kernels, local_forward(): pl.pallas_call(functools.partial(kernel, rows_n, cols_n), out_shape=jax.S...  125 us
    unnamed x1, local copies, waits for them, and re-layouts  4.64 us

profile of v2, /device:TPU:97, one launch (start us, length us, event | category | flops | bytes accessed | tf_op | source)
XLA Modules:
  0.0 130.7 jit_solution(13426017432379147079)
XLA Ops:
  0.0 1.3 reshape.25.w1
  1.3 124.7 %encoder.1 = bf16[256,32,256]{2,1,0:T(8,128)(2,1)} custom-call(bf16[128,2,8,256]{3,2,1,0:T(8,128)(2,1)} %bitcast.15, bf16[9,64]{1,0:T(8,128)(2,1)} %reshape.25.w1, f32[3,64]{1,0:T(4,128)} %v1.1, bf16[576,64]{1,0:T(8,128)(2,1)} %bitcast.18, f32[3,64]{1,0:T(4,128)} %u1_.1, bf16[576,128]{1,0:T(8,128)(2,1)} %bitcast.19, f32[3,128]{1,0:T(4,128)} %v2.1, ...), custom_call_target="tpu_custom_call" | custom-call | tf_op jit(solution)/shard_map/encoder/pallas_call | solution.py:484
  126.0 4.6 %copy.16 = bf16[256,32,1,256]{3,1,2,0:T(8,128)(2,1)} copy(bf16[256,32,1,256]{3,1,2,0:T(8,128)(2,1)} %bitcast.13) | data formatting | bytes 8388608

commit v3 on v2

--- a/solution.py
+++ b/solution.py
@@ -38,8 +38,7 @@
 
 
 def build_weights(w1_ref, r1_ref, d2_ref, r2_ref, m1, m2, m3, m4, cols):
-    taps = w1_ref[...].astype(F32)
-    taps = jnp.concatenate([taps] * 4, axis=1)
+    taps = [jnp.concatenate([w1_ref[t].astype(F32)] * 4, axis=1) for t in range(3)]
     shape = (2 * LANES, 2 * LANES)
     k, n = iota(shape, 0), iota(shape, 1)
     kk = rem(k, LANES)
@@ -56,7 +55,8 @@
         code = jnp.where(good, 3 * d_row + d_col, -1)
         total = jnp.zeros(shape, F32)
         for index in range(9):
-            total = jnp.where(code == index, taps[index:index + 1], total)
+            t, c = divmod(index, 3)
+            total = jnp.where(code == index, taps[t][c:c + 1], total)
         m1[block] = total.astype(BF16)
         return 0
 
@@ -77,6 +77,10 @@
     return jnp.where(div(rem(iota(shape, 0), period), group) == div(rem(iota(shape, 1), period), group), 1.0, 0.0).astype(F32)
 
 
+def relu16(value):
+    return jnp.maximum(value, 0.0).astype(BF16)
+
+
 def down_strip(row):
     return jnp.where(iota(row.shape, 0) == 0, 0.0, pltpu.roll(row, 1, 0))
 
@@ -107,6 +111,7 @@
         self.r3 = y3.shape[2] - 2
         self.sums = None
         self.squares = None
+        self.gate = None
 
     def lhs(self, parts):
         parts = [part.reshape(part.shape[0] * STRIPS, LANES) for part in parts]
@@ -116,7 +121,9 @@
         rows = summed.shape[0]
         summed = summed + bias
         cube = summed.reshape(rows // STRIPS, STRIPS, 2 * LANES)
-        sums, squares = jnp.sum(cube, axis=0), jnp.sum(cube * cube, axis=0)
+        square = cube * cube
+        self.marks = square[:, :, :LANES]
+        sums, squares = jnp.sum(cube, axis=0), jnp.sum(square, axis=0)
         self.sums = sums if self.sums is None else self.sums + sums
         self.squares = squares if self.squares is None else self.squares + squares
         self.acc[first, 0:rows] = summed[:, :LANES]
@@ -220,9 +227,19 @@
             pairs = [coefficients(sums[:, lo:lo + LANES], squares[:, lo:lo + LANES], folds, affine[1:2, lo:lo + LANES], affine[2:3, lo:lo + LANES], count) for lo in (0, LANES)]
             self.scale, self.shift = [pair[0] for pair in pairs], [pair[1] for pair in pairs]
 
+    def due(self, scale, rows):
+        if self.gate is None:
+            return jnp.broadcast_to(scale, (rows, STRIPS, LANES))
+        marks = self.gate
+        have = marks.shape[0]
+        if have > rows:
+            marks = marks.reshape(rows, have // rows, STRIPS, LANES)[:, 0]
+        elif have < rows:
+            marks = jnp.broadcast_to(marks[:, None], (have, rows // have, STRIPS, LANES)).reshape(rows, STRIPS, LANES)
+        return jnp.where(marks >= 0.0, scale, 0.0)
+
     def apply(self, block, rows, scale, shift):
-        cube = jnp.maximum(self.acc[block, 0:rows * STRIPS] * scale + shift, 0.0)
-        return cube.reshape(rows, STRIPS, LANES)
+        return self.acc[block, 0:rows * STRIPS].reshape(rows, STRIPS, LANES) * self.due(scale, rows) + shift
 
     def norm1(self):
         lane, q = iota((1, LANES), 1), self.q
@@ -235,11 +252,11 @@
             elif block == blocks - 1:
                 scale, shift = jnp.where(lane < 64, scale, 0.0), jnp.where(lane < 64, shift, 0.0)
             cube = self.apply(2 * block + parity, q, scale, shift)
-            self.y1[block, parity, 1:q + 1] = cube.astype(BF16)
+            self.y1[block, parity, 1:q + 1] = relu16(cube)
             if parity:
-                self.y1[block, 1, 0] = down_strip(cube[q - 1]).astype(BF16)
+                self.y1[block, 1, 0] = relu16(down_strip(cube[q - 1]))
             else:
-                self.y1[block, 0, q + 1] = up_strip(cube[0]).astype(BF16)
+                self.y1[block, 0, q + 1] = relu16(up_strip(cube[0]))
 
         return [functools.partial(piece, block, parity) for block in range(blocks) for parity in range(2)]
 
@@ -248,9 +265,9 @@
 
         def piece(block, parity):
             cube = self.apply(2 * block + parity, q, self.scale, self.shift)
-            self.z1[block + 1, parity, 1:q + 1] = cube.astype(BF16)
+            self.z1[block + 1, parity, 1:q + 1] = relu16(cube)
             if parity:
-                self.z1[block + 1, 1, 0] = down_strip(cube[q - 1]).astype(BF16)
+                self.z1[block + 1, 1, 0] = relu16(down_strip(cube[q - 1]))
 
         return [functools.partial(piece, block, parity) for block in range(self.cols // 4) for parity in range(2)]
 
@@ -259,9 +276,9 @@
 
         def piece(col):
             cube = self.apply(col, rows, self.scale, self.shift)
-            self.y2[col + 1, 1:rows + 1] = cube.astype(BF16)
-            self.y2[col + 1, 0] = down_strip(cube[rows - 1]).astype(BF16)
-            self.y2[col + 1, rows + 1] = up_strip(cube[0]).astype(BF16)
+            self.y2[col + 1, 1:rows + 1] = relu16(cube)
+            self.y2[col + 1, 0] = relu16(down_strip(cube[rows - 1]))
+            self.y2[col + 1, rows + 1] = relu16(up_strip(cube[0]))
 
         return [functools.partial(piece, col) for col in range(self.cols // 4)]
 
@@ -270,9 +287,9 @@
 
         def piece(col):
             cube = self.apply(col, 2 * rows, self.scale, self.shift).reshape(rows, 2, STRIPS, LANES)
-            self.z2[col + 1, 0, 1:rows + 1] = cube[:, 0].astype(BF16)
-            self.z2[col + 1, 1, 1:rows + 1] = cube[:, 1].astype(BF16)
-            self.z2[col + 1, 1, 0] = down_strip(cube[rows - 1, 1]).astype(BF16)
+            self.z2[col + 1, 0, 1:rows + 1] = relu16(cube[:, 0])
+            self.z2[col + 1, 1, 1:rows + 1] = relu16(cube[:, 1])
+            self.z2[col + 1, 1, 0] = relu16(down_strip(cube[rows - 1, 1]))
 
         return [functools.partial(piece, col) for col in range(self.cols // 4)]
 
@@ -281,9 +298,9 @@
 
         def piece(col, half):
             cube = self.apply(2 * col + half, rows, self.scale[half], self.shift[half])
-            self.y3[col + 1, half, 1:rows + 1] = cube.astype(BF16)
-            self.y3[col + 1, half, 0] = down_strip(cube[rows - 1]).astype(BF16)
-            self.y3[col + 1, half, rows + 1] = up_strip(cube[0]).astype(BF16)
+            self.y3[col + 1, half, 1:rows + 1] = relu16(cube)
+            self.y3[col + 1, half, 0] = relu16(down_strip(cube[rows - 1]))
+            self.y3[col + 1, half, rows + 1] = relu16(up_strip(cube[0]))
 
         return [functools.partial(piece, col, half) for col in range(self.cols // 8) for half in range(2)]
 
@@ -293,10 +310,11 @@
         per = STRIPS // row_parts
 
         def piece(col, half):
+            scale = self.due(self.scale[half], STRIPS)
             for strip in range(STRIPS):
                 part = self.acc[2 * col + half, pl.ds(strip, rows, stride=STRIPS), :]
-                part = jnp.maximum(part * self.scale[half] + self.shift[half], 0.0)
-                self.out[col * row_parts + strip // per, pl.ds((strip % per) * rows, rows), pl.ds(half * LANES, LANES)] = part.astype(BF16)
+                part = part * scale[strip] + self.shift[half]
+                self.out[col * row_parts + strip // per, pl.ds((strip % per) * rows, rows), pl.ds(half * LANES, LANES)] = relu16(part)
 
         return [functools.partial(piece, col, half) for col in range(self.cols // 8) for half in range(2)]
 
@@ -307,13 +325,29 @@
         return [self.norm1, self.norm2, self.norm3, self.norm4, self.norm5, self.norm6]
 
 
+def weave(conv, convs, norm, norms):
+    done = 0
+    groups = max(len(convs) - 1, 1)
+    for index, piece in enumerate(convs):
+        piece()
+        norm.gate = conv.marks
+        upto = min(index + 1, groups) * len(norms) // groups
+        for other in norms[done:upto]:
+            other()
+        done = upto
+    norm.gate = None
+
+
 def load_image(stage_ref, image, x):
     quads = x.shape[0] - 1
-    for quad in range(quads):
+
+    def piece(quad):
         row = stage_ref[image, pl.ds(quad, STRIPS, stride=quads), :]
         x[quad + 1] = row.astype(BF16)
         if quad == quads - 1:
             x[0] = down_strip(row).astype(BF16)
+
+    return [functools.partial(piece, quad) for quad in range(quads)]
 
 
 def zero_borders(z1, y2, z2, y3):
@@ -386,7 +420,8 @@
 
     lax.fori_loop(0, pair_n, send_pair, 0)
     build_weights(w1, r1, d2, r2, m1, m2, m3, m4, cols)
-    zero_borders(z1, y2, z2, y3)
+    for m in range(2):
+        zero_borders(z1.at[m], y2.at[m], z2.at[m], y3.at[m])
 
     def two(ref):
         row = ref[...]
@@ -408,17 +443,10 @@
             for m in range(2):
                 staged[m, pl.ds(row * quads, quads)] = turned[m * quads:(m + 1) * quads]
 
-        def one_image(m, _):
-            load_image(staged, m, x)
-            stream = Stream(mats, affines, acc, x, y1, z1, y2, z2, y3, out.at[m], cols)
-            for layer in range(6):
-                for piece in stream.convs()[layer]():
-                    piece()
-                stream.stats(layer)
-                if layer == 5:
-                    pl.when(pair > 0)(lambda: sent(m))
-                for piece in stream.norms()[layer]():
-                    piece()
+        def streams(m):
+            return Stream(mats, affines, acc.at[m], x.at[m], y1.at[m], z1.at[m], y2.at[m], z2.at[m], y3.at[m], out.at[m], cols)
+
+        def ship(m):
             image = (me * pair_n + pair) * 2 + m
             pltpu.make_async_copy(out.at[m, me], o_ref.at[image], out_own.at[m]).start()
 
@@ -430,9 +458,22 @@
                 return 0
 
             lax.fori_loop(1, devices, send, 0)
-            return 0
-
-        lax.fori_loop(0, 2, one_image, 0)
+
+        first, second = streams(0), streams(1)
+        for piece in load_image(staged, 0, x.at[0]):
+            piece()
+        for layer in range(6):
+            weave(first, first.convs()[layer](), second, second.norms()[layer - 1]() if layer else load_image(staged, 1, x.at[1]))
+            first.stats(layer)
+            if layer == 5:
+                pl.when(pair > 0)(lambda: sent(0))
+            weave(second, second.convs()[layer](), first, first.norms()[layer]())
+            second.stats(layer)
+        ship(0)
+        pl.when(pair > 0)(lambda: sent(1))
+        for piece in second.norms()[5]():
+            piece()
+        ship(1)
         return 0
 
     lax.fori_loop(0, pair_n, one_pair, 0)
@@ -457,7 +498,8 @@
         blocks = cols // 4 + 1
         r2, r3 = q, q // 2
         x = jnp.transpose(tile, (0, 3, 2, 1)).reshape(pairs, 2, tile_cols, rows)
-        flat = [param.reshape(-1, param.shape[-1]) for param in params]
+        flat = [jnp.transpose(params[0], (0, 2, 1, 3)).reshape(3, 3, -1)]
+        flat += [param.reshape(-1, param.shape[-1]) for param in params[1:]]
         scratch = [
             pltpu.VMEM((2 * rows, 2 * rows), BF16),
             pltpu.VMEM((pairs, 4 * tile_cols, LANES), BF16),
@@ -467,13 +509,13 @@
             pltpu.VMEM((16 * 64, 2 * LANES), BF16),
             pltpu.VMEM((18 * 64, 2 * LANES), BF16),
             pltpu.VMEM((12 * LANES, 2 * LANES), BF16),
-            pltpu.VMEM((2 * blocks, q * STRIPS, LANES), F32),
-            pltpu.VMEM((q + 1, STRIPS, LANES), BF16),
-            pltpu.VMEM((blocks, 2, q + 2, STRIPS, LANES), BF16),
-            pltpu.VMEM((blocks, 2, q + 1, STRIPS, LANES), BF16),
-            pltpu.VMEM((cols // 4 + 2, r2 + 2, STRIPS, LANES), BF16),
-            pltpu.VMEM((cols // 4 + 1, 2, r3 + 1, STRIPS, LANES), BF16),
-            pltpu.VMEM((cols // 8 + 2, 2, r3 + 2, STRIPS, LANES), BF16),
+            pltpu.VMEM((2, 2 * blocks, q * STRIPS, LANES), F32),
+            pltpu.VMEM((2, q + 1, STRIPS, LANES), BF16),
+            pltpu.VMEM((2, blocks, 2, q + 2, STRIPS, LANES), BF16),
+            pltpu.VMEM((2, blocks, 2, q + 1, STRIPS, LANES), BF16),
+            pltpu.VMEM((2, cols // 4 + 2, r2 + 2, STRIPS, LANES), BF16),
+            pltpu.VMEM((2, cols // 4 + 1, 2, r3 + 1, STRIPS, LANES), BF16),
+            pltpu.VMEM((2, cols // 8 + 2, 2, r3 + 2, STRIPS, LANES), BF16),
             pltpu.VMEM((2, devices, r3 * STRIPS // rows_n, 2 * LANES), BF16),
             pltpu.SemaphoreType.DMA,
             pltpu.SemaphoreType.DMA((pairs // devices,)),
@@ -483,12 +525,12 @@
         ]
         out = pl.pallas_call(
             functools.partial(kernel, rows_n, cols_n),
-            out_shape=jax.ShapeDtypeStruct((images, r3 * STRIPS // rows_n, 2 * LANES), BF16),
+            out_shape=pltpu.VMEM((images, r3 * STRIPS // rows_n, 2 * LANES), BF16),
             in_specs=[pl.BlockSpec(memory_space=pltpu.VMEM)] * 13,
             out_specs=pl.BlockSpec(memory_space=pl.ANY),
             scratch_shapes=scratch,
             name="encoder",
-            compiler_params=pltpu.CompilerParams(collective_id=0, has_side_effects=True, vmem_limit_bytes=56 * 1024 * 1024),
+            compiler_params=pltpu.CompilerParams(collective_id=0, has_side_effects=True, vmem_limit_bytes=59 * 1024 * 1024 + 900 * 1024),
         )(x, *flat)
         return out.reshape(images, out.shape[1], 1, 2 * LANES)
 

time: 131 us -> 125 us (0.954)
  local copies, waits for them, and re-layouts: 5.93 us -> 2.02 us
  Pallas kernels: 125 us -> 123 us
    unnamed x1, local copies, waits for them, and re-layouts: 4.64 us -> 2.02 us
    pallas_call x1, Pallas kernels: 125 us -> 123 us  [local_forward(): pl.pallas_call(functools.partial(kernel, rows_n, cols_n), out_shape=pltpu...]
where the time goes in v3:
time: 125 us
  Pallas kernels  123 us (98%)
  local copies, waits for them, and re-layouts  2.02 us (2%)
    pallas_call x1, Pallas kernels, local_forward(): pl.pallas_call(functools.partial(kernel, rows_n, cols_n), out_shape=pltpu...  123 us

profile of v3, /device:TPU:97, one launch (start us, length us, event | category | flops | bytes accessed | tf_op | source)
XLA Modules:
  0.0 124.9 jit_solution(4095382929199790725)
XLA Ops:
  0.0 122.9 %encoder.1 = bf16[256,32,256]{2,1,0:T(8,128)(2,1)S(1)} custom-call(bf16[128,2,8,256]{3,2,1,0:T(8,128)(2,1)} %bitcast.14, bf16[3,3,64]{2,1,0:T(4,128)(2,1)} %bitcast.19, f32[3,64]{1,0:T(4,128)} %v1.1, bf16[576,64]{1,0:T(8,128)(2,1)} %bitcast.17, f32[3,64]{1,0:T(4,128)} %u1_.1, bf16[576,128]{1,0:T(8,128)(2,1)} %bitcast.18, f32[3,128]{1,0:T(4,128)} %v2.1, ...), custom_call_target="tpu_custom_call" | custom-call | tf_op jit(solution)/shard_map/encoder/pallas_call | solution.py:526
  122.9 2.0 %copy.16 = bf16[256,32,1,256]{3,1,2,0:T(8,128)(2,1)} copy(bf16[256,32,1,256]{3,1,2,0:T(8,128)(2,1)S(1)} %bitcast.12) | data formatting | bytes 8388608

commit v4 on v3

--- a/solution.py
+++ b/solution.py
@@ -13,6 +13,9 @@
 BF16 = jnp.bfloat16
 LANES = 128
 STRIPS = 16
+SUB = 8
+WAIT = 1
+SPLIT = (1, 2, 4, 2, 2, 1)
 
 
 def iota(shape, dim):
@@ -117,8 +120,9 @@
         parts = [part.reshape(part.shape[0] * STRIPS, LANES) for part in parts]
         return jnp.concatenate(parts, axis=1)
 
-    def finish(self, summed, bias, first, second):
+    def finish(self, summed, bias, first, second, low=0, turned=False):
         rows = summed.shape[0]
+        at = pl.ds(low * STRIPS, rows)
         summed = summed + bias
         cube = summed.reshape(rows // STRIPS, STRIPS, 2 * LANES)
         square = cube * cube
@@ -126,8 +130,16 @@
         sums, squares = jnp.sum(cube, axis=0), jnp.sum(square, axis=0)
         self.sums = sums if self.sums is None else self.sums + sums
         self.squares = squares if self.squares is None else self.squares + squares
-        self.acc[first, 0:rows] = summed[:, :LANES]
-        self.acc[second, 0:rows] = summed[:, LANES:]
+        if turned:
+            cube = summed.reshape(rows // STRIPS, STRIPS // SUB, SUB, 2 * LANES)
+            half_rows = rows // STRIPS * SUB
+            for part in range(STRIPS // SUB):
+                flat = cube[:, part].reshape(half_rows, 2 * LANES)
+                self.acc[first, pl.ds(part * half_rows, half_rows)] = flat[:, :LANES]
+                self.acc[second, pl.ds(part * half_rows, half_rows)] = flat[:, LANES:]
+            return
+        self.acc[first, at] = summed[:, :LANES]
+        self.acc[second, at] = summed[:, LANES:]
 
     def two(self, row):
         return jnp.concatenate([row, row], axis=1)
@@ -152,63 +164,73 @@
     def conv2(self):
         bias, q = self.two(self.affines[1][0:1]), self.q
 
-        def piece(block):
+        step = q // SPLIT[1]
+
+        def piece(block, low):
             parts = []
             for parity, start in ((1, 0), (0, 1), (1, 1), (0, 2)):
                 for near in range(2):
-                    parts.append(self.y1[block + near, parity, start:start + q])
-            self.finish(jnp.dot(self.lhs(parts), self.mats[1][...], preferred_element_type=F32), bias, 2 * block, 2 * block + 1)
-
-        return [functools.partial(piece, block) for block in range(self.cols // 4)]
+                    parts.append(self.y1[block + near, parity, start + low:start + low + step])
+            self.finish(jnp.dot(self.lhs(parts), self.mats[1][...], preferred_element_type=F32), bias, 2 * block, 2 * block + 1, low)
+
+        return [functools.partial(piece, block, low) for block in range(self.cols // 4) for low in range(0, q, step)]
 
     def conv3(self):
         bias, q = self.two(self.affines[2][0:1]), self.q
 
-        def piece(block):
+        step = q // SPLIT[2]
+
+        def piece(block, low):
             parts = []
             for parity, start in ((1, 0), (0, 1), (1, 1)):
                 for near in range(3):
-                    parts.append(self.z1[2 * block + near, parity, start:start + q])
-            self.finish(jnp.dot(self.lhs(parts), self.mats[2][...], preferred_element_type=F32), bias, 2 * block, 2 * block + 1)
-
-        return [functools.partial(piece, block) for block in range(self.cols // 8)]
+                    parts.append(self.z1[2 * block + near, parity, start + low:start + low + step])
+            self.finish(jnp.dot(self.lhs(parts), self.mats[2][...], preferred_element_type=F32), bias, 2 * block, 2 * block + 1, low)
+
+        return [functools.partial(piece, block, low) for block in range(self.cols // 8) for low in range(0, q, step)]
 
     def conv4(self):
         bias = self.two(self.affines[3][0:1])
 
-        def piece(block):
+        step = self.r2 // SPLIT[3]
+
+        def piece(block, low):
             parts = []
             for start in range(3):
                 for near in range(4):
-                    parts.append(self.y2[2 * block + near, start:start + self.r2])
-            self.finish(jnp.dot(self.lhs(parts), self.mats[3][...], preferred_element_type=F32), bias, 2 * block, 2 * block + 1)
-
-        return [functools.partial(piece, block) for block in range(self.cols // 8)]
+                    parts.append(self.y2[2 * block + near, start + low:start + low + step])
+            self.finish(jnp.dot(self.lhs(parts), self.mats[3][...], preferred_element_type=F32), bias, 2 * block, 2 * block + 1, low)
+
+        return [functools.partial(piece, block, low) for block in range(self.cols // 8) for low in range(0, self.r2, step)]
 
     def conv5(self):
         bias = self.affines[4][0:1]
 
-        def piece(col):
+        step = self.r3 // SPLIT[4]
+
+        def piece(col, low):
             parts = []
             for parity, start in ((1, 0), (0, 1), (1, 1)):
                 for near in range(3):
-                    parts.append(self.z2[2 * col + near, parity, start:start + self.r3])
-            self.finish(jnp.dot(self.lhs(parts), self.mats[4][...], preferred_element_type=F32), bias, 2 * col, 2 * col + 1)
-
-        return [functools.partial(piece, col) for col in range(self.cols // 8)]
+                    parts.append(self.z2[2 * col + near, parity, start + low:start + low + step])
+            self.finish(jnp.dot(self.lhs(parts), self.mats[4][...], preferred_element_type=F32), bias, 2 * col, 2 * col + 1, low)
+
+        return [functools.partial(piece, col, low) for col in range(self.cols // 8) for low in range(0, self.r3, step)]
 
     def conv6(self):
         bias = self.affines[5][0:1]
 
-        def piece(col):
+        step = self.r3 // SPLIT[5]
+
+        def piece(col, low):
             parts = []
             for start in range(3):
                 for near in range(3):
                     for half in range(2):
-                        parts.append(self.y3[col + near, half, start:start + self.r3])
-            self.finish(jnp.dot(self.lhs(parts), self.mats[5][...], preferred_element_type=F32), bias, 2 * col, 2 * col + 1)
-
-        return [functools.partial(piece, col) for col in range(self.cols // 8)]
+                        parts.append(self.y3[col + near, half, start + low:start + low + step])
+            self.finish(jnp.dot(self.lhs(parts), self.mats[5][...], preferred_element_type=F32), bias, 2 * col, 2 * col + 1, turned=True)
+
+        return [functools.partial(piece, col, low) for col in range(self.cols // 8) for low in range(0, self.r3, step)]
 
     def stats(self, layer):
         affine = self.affines[layer]
@@ -312,7 +334,7 @@
         def piece(col, half):
             scale = self.due(self.scale[half], STRIPS)
             for strip in range(STRIPS):
-                part = self.acc[2 * col + half, pl.ds(strip, rows, stride=STRIPS), :]
+                part = self.acc[2 * col + half, pl.ds(strip // SUB * rows * SUB + strip % SUB, rows, stride=SUB), :]
                 part = part * scale[strip] + self.shift[half]
                 self.out[col * row_parts + strip // per, pl.ds((strip % per) * rows, rows), pl.ds(half * LANES, LANES)] = relu16(part)
 
@@ -325,13 +347,18 @@
         return [self.norm1, self.norm2, self.norm3, self.norm4, self.norm5, self.norm6]
 
 
-def weave(conv, convs, norm, norms):
+def weave(conv, convs, norm, norms, prepare=None):
     done = 0
-    groups = max(len(convs) - 1, 1)
+    start = min(WAIT, max(len(convs) - 3, 0))
+    groups = max(len(convs) - 1 - start, 1)
     for index, piece in enumerate(convs):
         piece()
+        if index < start:
+            continue
+        if index == start and prepare is not None:
+            prepare()
         norm.gate = conv.marks
-        upto = min(index + 1, groups) * len(norms) // groups
+        upto = min(index - start + 1, groups) * len(norms) // groups
         for other in norms[done:upto]:
             other()
         done = upto
@@ -342,7 +369,7 @@
     quads = x.shape[0] - 1
 
     def piece(quad):
-        row = stage_ref[image, pl.ds(quad, STRIPS, stride=quads), :]
+        row = stage_ref[image, pl.ds(quad // SUB * STRIPS * SUB + quad % SUB, STRIPS, stride=SUB), :]
         x[quad + 1] = row.astype(BF16)
         if quad == quads - 1:
             x[0] = down_strip(row).astype(BF16)
@@ -429,7 +456,7 @@
 
     affines = [two(v1), two(u1), v2[...], u2[...], v3[...], u3[...]]
     mats = [m1, m2, m3, m4, d3, r3]
-    quads = staged.shape[1] // rows_n
+    quads, per_strip = staged.shape[1] // rows_n, staged.shape[1] // STRIPS
 
     def sent(slot):
         part = out.at[slot, pl.ds(0, devices - 1)]
@@ -441,7 +468,10 @@
         for row in range(rows_n):
             turned = jnp.transpose(landed[pair, row].astype(F32).reshape(LANES, LANES))
             for m in range(2):
-                staged[m, pl.ds(row * quads, quads)] = turned[m * quads:(m + 1) * quads]
+                for part in range(quads // SUB):
+                    strip, eight = row * quads // per_strip + part * SUB // per_strip, part % (per_strip // SUB)
+                    low = m * quads + part * SUB
+                    staged[m, pl.ds((eight * STRIPS + strip) * SUB, SUB)] = turned[low:low + SUB]
 
         def streams(m):
             return Stream(mats, affines, acc.at[m], x.at[m], y1.at[m], z1.at[m], y2.at[m], z2.at[m], y3.at[m], out.at[m], cols)
@@ -463,12 +493,14 @@
         for piece in load_image(staged, 0, x.at[0]):
             piece()
         for layer in range(6):
-            weave(first, first.convs()[layer](), second, second.norms()[layer - 1]() if layer else load_image(staged, 1, x.at[1]))
-            first.stats(layer)
+            if layer:
+                weave(first, first.convs()[layer](), second, second.norms()[layer - 1](), functools.partial(second.stats, layer - 1))
+            else:
+                weave(first, first.convs()[0](), second, load_image(staged, 1, x.at[1]))
             if layer == 5:
                 pl.when(pair > 0)(lambda: sent(0))
-            weave(second, second.convs()[layer](), first, first.norms()[layer]())
-            second.stats(layer)
+            weave(second, second.convs()[layer](), first, first.norms()[layer](), functools.partial(first.stats, layer))
+        second.stats(5)
         ship(0)
         pl.when(pair > 0)(lambda: sent(1))
         for piece in second.norms()[5]():

time: 125 us -> 116 us (0.928)
  Pallas kernels: 123 us -> 113 us
    pallas_call x1, Pallas kernels: 123 us -> 113 us  [local_forward(): pl.pallas_call(functools.partial(kernel, rows_n, cols_n), out_shape=pltpu...]
where the time goes in v4:
time: 116 us; the launch traced here: 115 us
  Pallas kernels  113 us (97%)
  local copies, waits for them, and re-layouts  2.02 us (2%)
    pallas_call x1, Pallas kernels, local_forward(): pl.pallas_call(functools.partial(kernel, rows_n, cols_n), out_shape=pltpu...  113 us

profile of v4, /device:TPU:97, one launch (start us, length us, event | category | flops | bytes accessed | tf_op | source)
XLA Modules:
  0.0 115.5 jit_solution(5749650003960077577)
XLA Ops:
  0.0 113.5 %encoder.1 = bf16[256,32,256]{2,1,0:T(8,128)(2,1)S(1)} custom-call(bf16[128,2,8,256]{3,2,1,0:T(8,128)(2,1)} %bitcast.14, bf16[3,3,64]{2,1,0:T(4,128)(2,1)} %bitcast.19, f32[3,64]{1,0:T(4,128)} %v1.1, bf16[576,64]{1,0:T(8,128)(2,1)} %bitcast.17, f32[3,64]{1,0:T(4,128)} %u1_.1, bf16[576,128]{1,0:T(8,128)(2,1)} %bitcast.18, f32[3,128]{1,0:T(4,128)} %v2.1, ...), custom_call_target="tpu_custom_call" | custom-call | tf_op jit(solution)/shard_map/encoder/pallas_call | solution.py:558
  113.5 2.0 %copy.16 = bf16[256,32,1,256]{3,1,2,0:T(8,128)(2,1)} copy(bf16[256,32,1,256]{3,1,2,0:T(8,128)(2,1)S(1)} %bitcast.12) | data formatting | bytes 8388608

commit v5 on v4

--- a/solution.py
+++ b/solution.py
@@ -14,6 +14,8 @@
 LANES = 128
 STRIPS = 16
 SUB = 8
+WIDE = 256
+PHASES = ((1, 0), (0, 1), (1, 1))
 WAIT = 1
 SPLIT = (1, 2, 4, 2, 2, 1)
 
@@ -42,7 +44,7 @@
 
 def build_weights(w1_ref, r1_ref, d2_ref, r2_ref, m1, m2, m3, m4, cols):
     taps = [jnp.concatenate([w1_ref[t].astype(F32)] * 4, axis=1) for t in range(3)]
-    shape = (2 * LANES, 2 * LANES)
+    shape = (WIDE, WIDE)
     k, n = iota(shape, 0), iota(shape, 1)
     kk = rem(k, LANES)
     row = 4 * (div(k, LANES) - 1) + rem(div(kk, 8), 4)
@@ -124,51 +126,54 @@
         rows = summed.shape[0]
         at = pl.ds(low * STRIPS, rows)
         summed = summed + bias
-        cube = summed.reshape(rows // STRIPS, STRIPS, 2 * LANES)
+        cube = summed.reshape(rows // STRIPS, STRIPS, WIDE)
         square = cube * cube
         self.marks = square[:, :, :LANES]
         sums, squares = jnp.sum(cube, axis=0), jnp.sum(square, axis=0)
         self.sums = sums if self.sums is None else self.sums + sums
         self.squares = squares if self.squares is None else self.squares + squares
         if turned:
-            cube = summed.reshape(rows // STRIPS, STRIPS // SUB, SUB, 2 * LANES)
+            cube = summed.reshape(rows // STRIPS, STRIPS // SUB, SUB, WIDE)
             half_rows = rows // STRIPS * SUB
             for part in range(STRIPS // SUB):
-                flat = cube[:, part].reshape(half_rows, 2 * LANES)
+                flat = cube[:, part].reshape(half_rows, WIDE)
                 self.acc[first, pl.ds(part * half_rows, half_rows)] = flat[:, :LANES]
                 self.acc[second, pl.ds(part * half_rows, half_rows)] = flat[:, LANES:]
             return
         self.acc[first, at] = summed[:, :LANES]
         self.acc[second, at] = summed[:, LANES:]
 
+    def bias(self, layer):
+        return self.affines[layer][0:1]
+
     def two(self, row):
         return jnp.concatenate([row, row], axis=1)
 
     def conv1(self):
-        affine = self.affines[0]
+        row = self.bias(0)
         lane = iota((1, LANES), 1)
         blocks = self.mats[0].shape[0]
-        bias = self.two(affine[0:1])
+        bias = self.two(row)
 
         def piece(block):
             own = bias
             if block == 0:
-                own = self.two(jnp.where(lane < 64, 0.0, affine[0:1]))
+                own = self.two(jnp.where(lane < 64, 0.0, row))
             elif block == blocks - 1:
-                own = self.two(jnp.where(lane < 64, affine[0:1], 0.0))
+                own = self.two(jnp.where(lane < 64, row, 0.0))
             left = self.lhs([self.x[0:self.q], self.x[1:self.q + 1]])
             self.finish(jnp.dot(left, self.mats[0][block], preferred_element_type=F32), own, 2 * block, 2 * block + 1)
 
         return [functools.partial(piece, block) for block in range(blocks)]
 
     def conv2(self):
-        bias, q = self.two(self.affines[1][0:1]), self.q
+        bias, q = self.two(self.bias(1)), self.q
 
         step = q // SPLIT[1]
 
         def piece(block, low):
             parts = []
-            for parity, start in ((1, 0), (0, 1), (1, 1), (0, 2)):
+            for parity, start in PHASES + ((0, 2),):
                 for near in range(2):
                     parts.append(self.y1[block + near, parity, start + low:start + low + step])
             self.finish(jnp.dot(self.lhs(parts), self.mats[1][...], preferred_element_type=F32), bias, 2 * block, 2 * block + 1, low)
@@ -176,13 +181,13 @@
         return [functools.partial(piece, block, low) for block in range(self.cols // 4) for low in range(0, q, step)]
 
     def conv3(self):
-        bias, q = self.two(self.affines[2][0:1]), self.q
+        bias, q = self.two(self.bias(2)), self.q
 
         step = q // SPLIT[2]
 
         def piece(block, low):
             parts = []
-            for parity, start in ((1, 0), (0, 1), (1, 1)):
+            for parity, start in PHASES:
                 for near in range(3):
                     parts.append(self.z1[2 * block + near, parity, start + low:start + low + step])
             self.finish(jnp.dot(self.lhs(parts), self.mats[2][...], preferred_element_type=F32), bias, 2 * block, 2 * block + 1, low)
@@ -190,7 +195,7 @@
         return [functools.partial(piece, block, low) for block in range(self.cols // 8) for low in range(0, q, step)]
 
     def conv4(self):
-        bias = self.two(self.affines[3][0:1])
+        bias = self.two(self.bias(3))
 
         step = self.r2 // SPLIT[3]
 
@@ -204,13 +209,13 @@
         return [functools.partial(piece, block, low) for block in range(self.cols // 8) for low in range(0, self.r2, step)]
 
     def conv5(self):
-        bias = self.affines[4][0:1]
+        bias = self.bias(4)
 
         step = self.r3 // SPLIT[4]
 
         def piece(col, low):
             parts = []
-            for parity, start in ((1, 0), (0, 1), (1, 1)):
+            for parity, start in PHASES:
                 for near in range(3):
                     parts.append(self.z2[2 * col + near, parity, start + low:start + low + step])
             self.finish(jnp.dot(self.lhs(parts), self.mats[4][...], preferred_element_type=F32), bias, 2 * col, 2 * col + 1, low)
@@ -218,7 +223,7 @@
         return [functools.partial(piece, col, low) for col in range(self.cols // 8) for low in range(0, self.r3, step)]
 
     def conv6(self):
-        bias = self.affines[5][0:1]
+        bias = self.bias(5)
 
         step = self.r3 // SPLIT[5]
 
@@ -411,7 +416,7 @@
 
 
 def kernel(rows_n, cols_n, x_ref, w1, v1, r1, u1, d2, v2, r2, u2, d3, v3, r3, u3, o_ref, perm, packed, landed, staged,
-           m1, m2, m3, m4, acc, x, y1, z1, y2, z2, y3, out, in_send, in_recv, out_send, out_recv, out_own):
+           m1, m2, m3, m4, acc, x, y1, z1, y2, z2, y3, out, in_send, in_recv, out_send, out_recv, out_own, held, held_sem):
     devices = rows_n * cols_n
     my_row, my_col = lax.axis_index("h"), lax.axis_index("w")
     me = my_col * rows_n + my_row
@@ -429,6 +434,9 @@
         return 0
 
     lax.fori_loop(1, devices, greet, 0)
+    loads = [pltpu.make_async_copy(ref, held[n], held_sem.at[n]) for n, ref in enumerate((r1, d2, r2, d3, r3))]
+    for load in loads:
+        load.start()
     pack(x_ref, perm, packed)
     pl.semaphore_wait(barrier, devices - 1)
 
@@ -446,6 +454,9 @@
         return 0
 
     lax.fori_loop(0, pair_n, send_pair, 0)
+    for load in loads:
+        load.wait()
+    r1, d2, r2, d3, r3 = held
     build_weights(w1, r1, d2, r2, m1, m2, m3, m4, cols)
     for m in range(2):
         zero_borders(z1.at[m], y2.at[m], z2.at[m], y3.at[m])
@@ -500,8 +511,8 @@
             if layer == 5:
                 pl.when(pair > 0)(lambda: sent(0))
             weave(second, second.convs()[layer](), first, first.norms()[layer](), functools.partial(first.stats, layer))
+        ship(0)
         second.stats(5)
-        ship(0)
         pl.when(pair > 0)(lambda: sent(1))
         for piece in second.norms()[5]():
             piece()
@@ -529,41 +540,49 @@
         q = rows_n * rows // 4 // STRIPS
         blocks = cols // 4 + 1
         r2, r3 = q, q // 2
+        wide, narrow, rows3 = cols // 4, cols // 8, r3 * STRIPS // rows_n
+
+        def both(*shape):
+            return pltpu.VMEM((2, *shape), BF16)
+
         x = jnp.transpose(tile, (0, 3, 2, 1)).reshape(pairs, 2, tile_cols, rows)
         flat = [jnp.transpose(params[0], (0, 2, 1, 3)).reshape(3, 3, -1)]
         flat += [param.reshape(-1, param.shape[-1]) for param in params[1:]]
+        large = (2, 4, 6, 8, 10)
         scratch = [
             pltpu.VMEM((2 * rows, 2 * rows), BF16),
             pltpu.VMEM((pairs, 4 * tile_cols, LANES), BF16),
             pltpu.VMEM((pairs // devices, rows_n, cols_n, 4 * tile_cols, LANES), BF16),
             pltpu.VMEM((2, q * STRIPS, LANES), F32),
-            pltpu.VMEM((blocks, 2 * LANES, 2 * LANES), BF16),
-            pltpu.VMEM((16 * 64, 2 * LANES), BF16),
-            pltpu.VMEM((18 * 64, 2 * LANES), BF16),
-            pltpu.VMEM((12 * LANES, 2 * LANES), BF16),
+            pltpu.VMEM((blocks, WIDE, WIDE), BF16),
+            pltpu.VMEM((16 * 64, WIDE), BF16),
+            pltpu.VMEM((18 * 64, WIDE), BF16),
+            pltpu.VMEM((12 * LANES, WIDE), BF16),
             pltpu.VMEM((2, 2 * blocks, q * STRIPS, LANES), F32),
-            pltpu.VMEM((2, q + 1, STRIPS, LANES), BF16),
-            pltpu.VMEM((2, blocks, 2, q + 2, STRIPS, LANES), BF16),
-            pltpu.VMEM((2, blocks, 2, q + 1, STRIPS, LANES), BF16),
-            pltpu.VMEM((2, cols // 4 + 2, r2 + 2, STRIPS, LANES), BF16),
-            pltpu.VMEM((2, cols // 4 + 1, 2, r3 + 1, STRIPS, LANES), BF16),
-            pltpu.VMEM((2, cols // 8 + 2, 2, r3 + 2, STRIPS, LANES), BF16),
-            pltpu.VMEM((2, devices, r3 * STRIPS // rows_n, 2 * LANES), BF16),
+            both(q + 1, STRIPS, LANES),
+            both(blocks, 2, q + 2, STRIPS, LANES),
+            both(blocks, 2, q + 1, STRIPS, LANES),
+            both(wide + 2, r2 + 2, STRIPS, LANES),
+            both(wide + 1, 2, r3 + 1, STRIPS, LANES),
+            both(narrow + 2, 2, r3 + 2, STRIPS, LANES),
+            both(devices, rows3, WIDE),
             pltpu.SemaphoreType.DMA,
             pltpu.SemaphoreType.DMA((pairs // devices,)),
             pltpu.SemaphoreType.DMA((2,)),
             pltpu.SemaphoreType.DMA,
             pltpu.SemaphoreType.DMA((2,)),
+            [pltpu.VMEM(flat[n].shape, BF16) for n in large],
+            pltpu.SemaphoreType.DMA((len(large),)),
         ]
         out = pl.pallas_call(
             functools.partial(kernel, rows_n, cols_n),
-            out_shape=pltpu.VMEM((images, r3 * STRIPS // rows_n, 2 * LANES), BF16),
-            in_specs=[pl.BlockSpec(memory_space=pltpu.VMEM)] * 13,
+            out_shape=pltpu.VMEM((images, rows3, WIDE), BF16),
+            in_specs=[pl.BlockSpec(memory_space=pl.ANY if n - 1 in large else pltpu.VMEM) for n in range(len(flat) + 1)],
             out_specs=pl.BlockSpec(memory_space=pl.ANY),
             scratch_shapes=scratch,
             name="encoder",
             compiler_params=pltpu.CompilerParams(collective_id=0, has_side_effects=True, vmem_limit_bytes=59 * 1024 * 1024 + 900 * 1024),
         )(x, *flat)
-        return out.reshape(images, out.shape[1], 1, 2 * LANES)
+        return out.reshape(images, out.shape[1], 1, WIDE)
 
     return jax.shard_map(local_forward, mesh=mesh, in_specs=(act_spec,) + (P(),) * 12, out_specs=act_spec, check_vma=False)

time: 116 us -> 115 us (level)
  no operation moved by 1% of the time
where the time goes in v5:
time: 115 us
  Pallas kernels  113 us (98%)
  local copies, waits for them, and re-layouts  2.02 us (2%)
    pallas_call x1, Pallas kernels, local_forward(): pl.pallas_call(functools.partial(kernel, rows_n, cols_n), out_shape=pltpu...  113 us

profile of v5, /device:TPU:97, one launch (start us, length us, event | category | flops | bytes accessed | tf_op | source)
XLA Modules:
  0.0 114.8 jit_solution(12378068176360943747)
XLA Ops:
  0.0 112.8 %encoder.1 = bf16[256,32,256]{2,1,0:T(8,128)(2,1)S(1)} custom-call(bf16[128,2,8,256]{3,2,1,0:T(8,128)(2,1)} %bitcast.14, bf16[3,3,64]{2,1,0:T(4,128)(2,1)} %bitcast.19, f32[3,64]{1,0:T(4,128)} %v1.1, bf16[576,64]{1,0:T(8,128)(2,1)} %bitcast.17, f32[3,64]{1,0:T(4,128)} %u1_.1, bf16[576,128]{1,0:T(8,128)(2,1)} %bitcast.18, f32[3,128]{1,0:T(4,128)} %v2.1, ...), custom_call_target="tpu_custom_call" | custom-call | tf_op jit(solution)/shard_map/encoder/pallas_call | solution.py:577
  112.8 2.0 %copy.16 = bf16[256,32,1,256]{3,1,2,0:T(8,128)(2,1)} copy(bf16[256,32,1,256]{3,1,2,0:T(8,128)(2,1)S(1)} %bitcast.12) | data formatting | bytes 8388608
